TPU v7x, 32 devices: a whole 2x2x4 slice. The times are simulated.
32 devices in a mesh: seq: 8 (over z, y), head: 4 (over x, core).
Axes of the slice: x: 2, y: 2, z: 4, core: 2. Of those that a mesh axis runs over, the one named last changes fastest.
Arguments:
- byte_input: float32 [3072, 2048], P('seq', 'head'), may hold values from -6 to 6
- b_proj: float32 [3072, 128], P('seq'), may hold values from -1.25 to 1.25
- c_proj: float32 [3072, 128], P('seq'), may hold values from -1.25 to 1.25
- step_decay: float32 [32, 3072], P('head', 'seq'), may hold values from 0 to 1
- skip_gain: float32 [32], P('head'), may hold values from 0.5 to 1.5
- out_weight: bfloat16 [2048, 1024], P('head'), may hold values from -0.125 to 0.125
- boundaries: int32 [8, 128], P('seq'), may hold values from 0 to 383, as said below
- counts: int32 [8], P('seq'), may hold values from 0 to 128, as said below
- norm_gain: float32 [1024], replicated, may hold values from 0.1 to 1.9
- qkv_weight: bfloat16 [3, 1024, 2048], P(None, None, 'head'), may hold values from -1 to 1
Outputs:
- attended: float32 [512, 2048], P('seq', 'head')
Inputs may be any that keep to these rules, and one draw needn't show every extreme that they name: `boundaries`: row s holds counts[s] strictly increasing offsets, then zeros. The counts sum to 512; for every shard s the sum of the counts of shards before s lies within 32 of s * 64; some shard has 128.
All inputs are finite; a program needn't handle non-finite values.
Results may differ from a plain program's by a relative error of at most 0.0075.
Values may be sent and summed in bfloat16 or wider, within the bound.
A program may use at most 128 MiB of HBM per device.

v0:
```python
import functools

import jax
import jax.numpy as jnp
from jax import lax
from jax.experimental import pallas as pl
from jax.experimental.pallas import tpu as pltpu
from jax.sharding import PartitionSpec as P

ATT_DIM = 64
ROWS_DEV = 64


def prefix(shard, axis, combine, identity):
    length, here = (lax.axis_size(axis), lax.axis_index(axis))
    everything = jax.tree.map(lambda part: lax.all_gather(part, axis), shard)
    start = jax.tree.map(
        lambda part, zero: jnp.broadcast_to(jnp.asarray(zero, part.dtype), part.shape),
        shard,
        identity,
    )

    def lap(k, before):
        reached = k < here
        new = combine(before, jax.tree.map(lambda part: part[k], everything))
        return jax.tree.map(lambda a, b: jnp.where(reached, a, b), new, before)

    return lax.fori_loop(0, length, lap, start)


def extended(cells, sides, width):
    for axis, dim in sides:
        count = lax.axis_size(axis)
        ends = count - 1
        head = lax.slice_in_dim(cells, 0, width, axis=dim)
        tail = lax.slice_in_dim(cells, cells.shape[dim] - width, cells.shape[dim], axis=dim)
        cells = jnp.concatenate(
            [
                lax.ppermute(tail, axis, [(i, (i + 1) % count) for i in range(ends)]),
                cells,
                lax.ppermute(head, axis, [((i + 1) % count, i) for i in range(ends)]),
            ],
            axis=dim,
        )
    return cells


def state_space(inputs, b_rows, c_rows, decay):
    log_decay = jnp.cumsum(-decay, axis=1)
    affinity = jnp.dot(c_rows, b_rows.T, precision=lax.Precision.HIGHEST)
    length = inputs.shape[0]
    causal = lax.broadcasted_iota(jnp.int32, (length, length), 0) >= lax.broadcasted_iota(
        jnp.int32, (length, length), 1
    )

    def one_head(pair):
        values, logs = pair
        weights = (
            jnp.where(causal, jnp.exp(jnp.where(causal, logs[:, None] - logs[None, :], 0.0)), 0.0)
            * affinity
        )
        return jnp.dot(weights, values, precision=lax.Precision.HIGHEST)

    inside = lax.map(one_head, (inputs.transpose(1, 0, 2), log_decay))
    tail = jnp.exp(log_decay[:, -1:] - log_decay)
    own_state = jnp.einsum("ht,thp,tn->hpn", tail, inputs, b_rows, precision=lax.Precision.HIGHEST)
    return (log_decay, inside, own_state)


def link(earlier, later):
    return (earlier[0] * later[0], later[0][:, None, None] * earlier[1] + later[1])


def body(
    byte_input,
    b_proj,
    c_proj,
    step_decay,
    skip_gain,
    out_weight,
    boundaries,
    counts,
    norm_gain,
    qkv_weight,
):
    heads_here = step_decay.shape[0]
    length = byte_input.shape[0]
    inputs = byte_input.reshape(length, heads_here, -1)
    log_decay, inside, own_state = state_space(inputs, b_proj, c_proj, step_decay)
    span_decay = jnp.exp(log_decay[:, -1])
    arriving = prefix(
        (span_decay, own_state), "seq", link, (jnp.ones_like(span_decay), jnp.zeros_like(own_state))
    )
    carried = jnp.exp(log_decay)[:, :, None] * jnp.einsum(
        "tn,hpn->htp", c_proj, arriving[1], precision=lax.Precision.HIGHEST
    )
    mixed_heads = inside + carried + skip_gain[:, None, None] * inputs.transpose(1, 0, 2)
    slots = boundaries.shape[1]
    picked = jnp.take(mixed_heads, boundaries[0], axis=1)
    selected = picked.transpose(1, 0, 2).reshape(slots, -1).astype(jnp.bfloat16)
    all_counts = lax.all_gather(counts, "seq", axis=0, tiled=True)
    starts = jnp.cumsum(all_counts) - all_counts
    myself = lax.axis_index("seq")
    shards = lax.axis_size("seq")
    slot = jnp.arange(slots, dtype=jnp.int32)

    def slot_index(source):
        inside_axis = (source >= 0) & (source < shards)
        safe = jnp.clip(source, 0, shards - 1)
        begin = jnp.take(starts, safe)
        number = jnp.take(all_counts, safe)
        return jnp.where(inside_axis & (slot < number), begin + slot, -1)

    global_index = jnp.concatenate(
        [slot_index(myself - 1), slot_index(myself), slot_index(myself + 1)]
    )
    first_row = myself * ROWS_DEV
    target = first_row + jnp.arange(ROWS_DEV, dtype=jnp.int32)
    picker = global_index[None, :] == target[:, None]
    nearby = extended(selected, (("seq", 0),), slots)
    owned = jnp.dot(picker.astype(jnp.bfloat16), nearby, preferred_element_type=jnp.float32).astype(
        jnp.bfloat16
    )
    partial_value = jnp.dot(owned, out_weight, preferred_element_type=jnp.float32)
    packed = lax.psum(partial_value, "head")
    normed = (
        packed * lax.rsqrt(jnp.mean(packed * packed, axis=-1, keepdims=True) + 1e-05) * norm_gain
    ).astype(jnp.bfloat16)
    query = jnp.dot(normed, qkv_weight[0], preferred_element_type=jnp.float32).astype(jnp.bfloat16)
    keyed = jnp.dot(normed, qkv_weight[1], preferred_element_type=jnp.float32).astype(jnp.bfloat16)
    valued = jnp.dot(normed, qkv_weight[2], preferred_element_type=jnp.float32).astype(jnp.bfloat16)
    att_here = query.shape[1] // ATT_DIM
    queries = query.reshape(ROWS_DEV, att_here, ATT_DIM)
    row_place = first_row + jnp.arange(ROWS_DEV, dtype=jnp.int32)
    scale = ATT_DIM ** (-0.5)
    running = jnp.full((att_here, ROWS_DEV), -1e30, jnp.float32)
    key_piece = lax.all_gather(keyed, "seq", axis=0, tiled=True)
    value_piece = lax.all_gather(valued, "seq", axis=0, tiled=True)
    count = key_piece.shape[0]
    key_heads = key_piece.reshape(count, att_here, ATT_DIM)
    value_heads = value_piece.reshape(count, att_here, ATT_DIM)
    scores = (
        jnp.einsum("qhd,khd->hqk", queries, key_heads, preferred_element_type=jnp.float32) * scale
    )
    allowed = jnp.arange(count, dtype=jnp.int32)[None, :] <= row_place[:, None]
    scores = jnp.where(allowed[None], scores, -1e30)
    highest = jnp.maximum(running, jnp.max(scores, axis=-1))
    exps = jnp.where(allowed[None], jnp.exp(scores - highest[:, :, None]), 0.0)
    totals = jnp.sum(exps, axis=-1)
    weights = exps.astype(jnp.bfloat16)
    accum = jnp.einsum("hqk,khd->hqd", weights, value_heads, preferred_element_type=jnp.float32)
    running, totals, accum = (highest, totals, accum)
    result = accum / totals[:, :, None]
    return result.transpose(1, 0, 2).reshape(ROWS_DEV, att_here * ATT_DIM)


F32 = jnp.float32
BF16 = jnp.bfloat16
STATE_WIRE = jnp.bfloat16
PART_WIRE = jnp.bfloat16
OUT_WIRE = jnp.bfloat16
EXTRA = 16


def exact_dot(a, b, dims=((1,), (0,))):
    return lax.dot_general(
        a, b, (dims, ((), ())), precision=lax.Precision.HIGHEST, preferred_element_type=F32
    )


def fast_dot(a, b, dims=((1,), (0,))):
    return lax.dot_general(a, b, (dims, ((), ())), preferred_element_type=F32)


def halves(a):
    high = a.astype(BF16)
    return high, (a - high.astype(F32)).astype(BF16)


def iota(shape, dim):
    return lax.broadcasted_iota(jnp.int32, shape, dim)


def fused(
    seqs,
    groups,
    decay_hbm,
    x_hbm,
    b_hbm,
    counts_hbm,
    bound_hbm,
    c_hbm,
    skip_hbm,
    outw_hbm,
    gain_hbm,
    qkvw_hbm,
    out_ref,
    decay_ref,
    x_ref,
    b_ref,
    counts_ref,
    bound_ref,
    c_ref,
    skip_ref,
    outw,
    gain_ref,
    qkvw,
    send_a,
    recv_a,
    send_b,
    recv_b,
    send_p,
    recv_p,
    recv_n,
    send_q,
    recv_q,
    send_o,
    recv_o,
    weight_sem,
    a_sem,
    b_sem,
    p_send,
    p_recv,
    n_sem,
    q_sem,
    o_sem,
):
    me = lax.axis_index("seq")
    col = lax.axis_index("head")
    length, width = x_ref.shape
    heads = decay_ref.shape[0]
    lanes = width // heads
    state = b_ref.shape[1]
    slots = bound_ref.shape[1]
    rows = out_ref.shape[0]
    piece = rows // groups
    half = rows // 2

    def shard_at(d):
        return lax.rem(me + d + seqs, seqs)

    layers = seqs // 2
    mid = layers // 2
    layer, side = me // 2, lax.rem(me, 2)
    near_end = layer < mid
    far_layers = [jnp.where(near_end, layers - 1 - k, k) for k in range(layers - mid)]
    same = jnp.where(near_end, layer, layer - (layers - mid))
    for k in range(1, mid):
        turn = lax.rem(same + k, mid)
        far_layers.append(jnp.where(near_end, turn, turn + (layers - mid)))
    targets = []
    for there in far_layers + [layer]:
        targets.append(2 * there + 1 - side)
        if there is not layer:
            targets.append(2 * there + side)

    def head_at(d):
        return lax.rem(col + d, groups)

    barrier = pltpu.get_barrier_semaphore()
    peers = [(shard_at(d), col) for d in range(1, seqs)]
    peers += [(me, head_at(d)) for d in range(1, groups)]
    peers += [(shard_at(e), head_at(d)) for e in (-1, 1) for d in range(1, groups)]
    for peer in peers:
        pl.semaphore_signal(
            barrier, inc=1, device_id=peer, device_id_type=pl.DeviceIdType.MESH
        )

    def remote(src, dst, sems, k, source, peer):
        return pltpu.make_async_remote_copy(
            src_ref=src,
            dst_ref=dst,
            send_sem=sems.at[0, k],
            recv_sem=sems.at[1, source],
            device_id=peer,
            device_id_type=pl.DeviceIdType.MESH,
        )

    loads = [
        pltpu.make_async_copy(source, target, weight_sem.at[i])
        for i, (source, target) in enumerate(
            (
                (decay_hbm, decay_ref),
                (x_hbm, x_ref),
                (b_hbm, b_ref),
                (counts_hbm, counts_ref),
                (bound_hbm, bound_ref),
                (c_hbm, c_ref),
                (skip_hbm, skip_ref),
                (outw_hbm, outw),
                (gain_hbm, gain_ref),
                (qkvw_hbm, qkvw),
            )
        )
    ]
    for load in loads[:7]:
        load.start()

    loads[0].wait()
    decay = decay_ref[...]
    upper = (iota((length, length), 0) <= iota((length, length), 1)).astype(F32)
    lower = (iota((length, length), 0) >= iota((length, length), 1)).astype(F32)
    logs = -exact_dot(decay, upper)
    logs_t = -exact_dot(lower, decay, ((1,), (1,)))
    first = iota((heads, width), 0) * lanes
    channel = iota((heads, width), 1)
    spread = ((channel >= first) & (channel < first + lanes)).astype(F32)
    tail_t = jnp.exp(logs_t[length - 1 : length, :] - logs_t)
    loads[1].wait()
    loads[2].wait()
    loads[3].wait()
    for load in loads[7:]:
        load.start()
    scaled = x_ref[...] * exact_dot(tail_t, spread)
    own = exact_dot(scaled, b_ref[...], ((0,), (0,)))
    number = jnp.broadcast_to(counts_ref[...].astype(F32), (EXTRA, state))
    extra_row = iota((EXTRA, state), 0)
    for h in range(heads):
        send_a[h, :lanes, :] = own[h * lanes : (h + 1) * lanes, :].astype(send_a.dtype)
        last = jnp.broadcast_to(logs[h : h + 1, length - 1 : length], (EXTRA, state))
        last_high, rest = halves(last)
        rest = last - last_high.astype(F32)
        last_mid, last_low = halves(rest)
        extra = jnp.where(extra_row == 1, last_mid.astype(F32), last_high.astype(F32))
        extra = jnp.where(extra_row == 2, last_low.astype(F32), extra)
        extra = jnp.where(extra_row == 3, number, extra)
        send_a[h, lanes:, :] = extra.astype(send_a.dtype)
    pl.semaphore_wait(barrier, len(peers))
    for to in targets:
        remote(send_a.at[to], recv_a.at[me], a_sem, to, me, (to, col)).start()
    recv_a[me] = send_a[me]

    for load in loads[4:7]:
        load.wait()
    marks = jnp.broadcast_to(bound_ref[...].astype(F32), (slots, slots)).T
    marks = jnp.concatenate([marks] * (length // slots), axis=1)
    place = iota((slots, length), 1).astype(F32)
    hit = place == marks
    seen = place <= marks
    onehot = hit.astype(F32)
    c_rows = exact_dot(onehot, c_ref[...])
    logs_sel = exact_dot(onehot, logs_t)
    affinity = exact_dot(c_rows, b_ref[...], ((1,), (1,)))
    inside = []
    first_lane = iota((slots, 2 * lanes), 1) < lanes
    for pair in range(heads // 2):
        x_high, x_low = halves(x_ref[:, pair * 2 * lanes : (pair + 1) * 2 * lanes])
        x_both = jnp.concatenate([x_high, x_low], axis=1)
        parts = []
        for h in (2 * pair, 2 * pair + 1):
            gap = logs_sel[:, h : h + 1] - logs[h : h + 1, :]
            weights = jnp.where(seen, jnp.exp(jnp.where(seen, gap, 0.0)), 0.0) * affinity
            weights = weights + jnp.where(hit, skip_ref[:, h : h + 1], 0.0)
            w_high, w_low = halves(weights)
            wide = fast_dot(w_high, x_both)
            parts.append(
                wide[:, : 2 * lanes] + wide[:, 2 * lanes :] + fast_dot(w_low, x_high)
            )
        inside.append(jnp.where(first_lane, parts[0], parts[1]))
    inside = jnp.concatenate(inside, axis=1)
    enter_scale = exact_dot(jnp.exp(logs_sel), spread)

    for d in range(1, seqs):
        source = shard_at(-d)
        copy = remote(send_a.at[shard_at(d)], recv_a.at[source], a_sem, source, source, (source, col))
        copy.wait_recv()
    running = jnp.zeros((lanes, state), F32)
    for s in range(seqs):
        send_b[s] = running.astype(send_b.dtype)
        if s < seqs - 1:
            tags = recv_a[s, lanes:, :].astype(F32)
            kept = jnp.exp((tags[0:1] + tags[1:2]) + tags[2:3])
            running = kept * running + recv_a[s, :lanes, :].astype(F32)
    for to in targets:
        remote(send_b.at[to], recv_b.at[me], b_sem, to, me, (to, col)).start()
    recv_b[me] = send_b[me]

    start = jnp.zeros((1, state), F32)
    for s in range(seqs):
        start = start + jnp.where(s < me, recv_a[s, lanes:, :].astype(F32)[3:4], 0.0)
    offset = start - (me * rows - half).astype(F32)
    slot = iota((slots, slots), 1).astype(F32)
    mine = jnp.broadcast_to(counts_ref[...].astype(F32), (slots, slots))
    shift = (slot == iota((slots, slots), 0).astype(F32) - offset) & (slot < mine)
    shift = shift.astype(BF16)

    for d in range(1, seqs):
        source = shard_at(-d)
        remote(send_b.at[shard_at(d)], recv_b.at[source], b_sem, source, source, (source, col)).wait_recv()
    entering = recv_b[...].reshape(heads * lanes, state)
    c_high, c_low = halves(c_rows)
    last_dims = ((1,), (1,))
    carried = fast_dot(c_high, entering, last_dims) + fast_dot(c_low, entering, last_dims)
    y = (inside + enter_scale * carried).astype(BF16)
    window = fast_dot(shift, y).astype(BF16)
    loads[7].wait()
    partial = fast_dot(window, outw[...])
    pieces = slots // piece
    for i in range(pieces):
        send_p[i] = partial[i * piece : (i + 1) * piece, :].astype(send_p.dtype)
    outer = (pieces - groups) // 2

    def project(src, slot, k, peer):
        return pltpu.make_async_remote_copy(
            src_ref=send_p.at[src],
            dst_ref=recv_p.at[slot],
            send_sem=p_send.at[k],
            recv_sem=p_recv.at[slot],
            device_id=peer,
            device_id_type=pl.DeviceIdType.MESH,
        )

    below_sent = [project(i, groups + col, i, (shard_at(-1), groups - outer + i)) for i in range(outer)]
    above_sent = [
        project(outer + groups + i, groups + col, outer + i, (shard_at(1), i))
        for i in range(outer)
    ]
    sent = []
    for d in range(1, groups):
        to = head_at(d)
        sent.append(project(outer + to, col, 2 * outer + d - 1, (me, to)))
    has_below, has_above = me > 0, me < seqs - 1

    @pl.when(has_below)
    def _():
        for copy in below_sent:
            copy.start()

    @pl.when(has_above)
    def _():
        for copy in above_sent:
            copy.start()

    for copy in sent:
        copy.start()
    recv_p[col] = send_p[outer + col]
    expects = (has_below & (col < outer)) | (has_above & (col >= outer))

    @pl.when(expects)
    def _():
        for k in range(groups):
            project(0, groups + k, 0, (shard_at(1), k)).wait_recv()

    @pl.when(jnp.logical_not(expects))
    def _():
        recv_p[groups:] = jnp.zeros((groups, piece, recv_p.shape[2]), recv_p.dtype)

    for d in range(1, groups):
        source = head_at(groups - d)
        project(0, source, 0, (me, source)).wait_recv()
    loads[8].wait()
    mixed = recv_p[0].astype(F32)
    for k in range(1, 2 * groups):
        mixed = mixed + recv_p[k].astype(F32)
    square = jnp.mean(mixed * mixed, axis=-1, keepdims=True)
    normed = (mixed * lax.rsqrt(square + 1e-05) * gain_ref[...]).astype(BF16)
    recv_n[col] = normed
    sent_n = []
    for d in range(1, groups):
        to = head_at(d)
        sent_n.append(remote(recv_n.at[col], recv_n.at[col], n_sem, to, col, (me, to)))
        sent_n[-1].start()
    for d in range(1, groups):
        source = head_at(groups - d)
        remote(recv_n.at[col], recv_n.at[source], n_sem, source, source, (me, source)).wait_recv()
    normed = recv_n[...].reshape(rows, -1)
    loads[9].wait()
    query, key, value = [
        fast_dot(normed, qkvw[i]).astype(BF16).astype(F32) for i in range(3)
    ]
    pair_width = 2 * lanes
    left = iota((rows, pair_width), 1) < lanes
    left_half = left[:half]

    def turned(a):
        return pltpu.roll(a, lanes, 1)

    for pair in range(heads // 2):
        at = slice(pair * pair_width, (pair + 1) * pair_width)
        q, k, v = query[:, at], key[:, at], value[:, at]
        send_q[2 * pair, :rows, :] = jnp.where(left, q, turned(k)).astype(BF16)
        send_q[2 * pair + 1, :rows, :] = jnp.where(left, turned(q), k).astype(BF16)
        above, below = v[:half], v[half:]
        send_q[2 * pair, rows:, :] = jnp.where(left_half, above, turned(below)).astype(BF16)
        send_q[2 * pair + 1, rows:, :] = jnp.where(
            left_half, turned(above), below
        ).astype(BF16)
    for to in targets:
        remote(send_q.at[to], recv_q.at[me], q_sem, to, me, (to, col)).start()
    recv_q[me] = send_q[me]
    for d in range(1, seqs):
        source = shard_at(-d)
        remote(send_q.at[shard_at(d)], recv_q.at[source], q_sem, source, source, (source, col)).wait_recv()
    coarse = seqs * rows
    both = recv_q[:, :rows, :].reshape(coarse, pair_width)
    wide = both.astype(F32)
    left_all = iota((coarse, pair_width), 1) < lanes
    queries = jnp.where(left_all, wide, 0.0).astype(BF16)
    keys = turned(wide).astype(BF16)
    values = []
    for s in range(seqs):
        packed = recv_q[s, rows:, :].astype(F32)
        values += [packed, turned(packed)]
    values = jnp.concatenate(values, axis=0).astype(BF16)
    scores = fast_dot(queries, keys, ((1,), (1,))) * (lanes ** (-0.5))
    allowed = iota((coarse, coarse), 0) >= iota((coarse, coarse), 1)
    scores = jnp.where(allowed, scores, -1e30)
    highest = jnp.max(scores, axis=-1, keepdims=True)
    exps = jnp.where(allowed, jnp.exp(scores - highest), 0.0)
    total = jnp.sum(exps, axis=-1, keepdims=True)
    result = fast_dot(exps.astype(BF16), values) / total
    for s in range(seqs):
        above = result[s * rows : s * rows + half]
        below = result[s * rows + half : (s + 1) * rows]
        send_o[s] = jnp.where(left_half, above, turned(below)).astype(send_o.dtype)
    for to in targets:
        remote(send_o.at[to], recv_o.at[me], o_sem, to, me, (to, col)).start()
    recv_o[me] = send_o[me]
    for d in range(1, seqs):
        source = shard_at(-d)
        remote(send_o.at[shard_at(d)], recv_o.at[source], o_sem, source, source, (source, col)).wait_recv()
    for pair in range(heads // 2):
        at = slice(pair * pair_width, (pair + 1) * pair_width)
        even, odd = recv_o[2 * pair].astype(F32), recv_o[2 * pair + 1].astype(F32)
        out_ref[:half, at] = jnp.where(left_half, even, turned(odd)).astype(OUT_WIRE)
        out_ref[half:, at] = jnp.where(left_half, turned(even), odd).astype(OUT_WIRE)

    for copy in sent + sent_n:
        copy.wait_send()

    @pl.when(has_below)
    def _():
        for copy in below_sent:
            copy.wait_send()

    @pl.when(has_above)
    def _():
        for copy in above_sent:
            copy.wait_send()

    for sems, send, recv in (
        (a_sem, send_a, recv_a),
        (b_sem, send_b, recv_b),
        (q_sem, send_q, recv_q),
        (o_sem, send_o, recv_o),
    ):
        for d in range(1, seqs):
            to = shard_at(d)
            remote(send.at[to], recv.at[me], sems, to, me, (to, col)).wait_send()


def fused_body(
    byte_input,
    b_proj,
    c_proj,
    step_decay,
    skip_gain,
    out_weight,
    boundaries,
    counts,
    norm_gain,
    qkv_weight,
):
    seqs, groups = lax.axis_size("seq"), lax.axis_size("head")
    heads = step_decay.shape[0]
    width = byte_input.shape[1]
    lanes = width // heads
    state = b_proj.shape[1]
    rows = ROWS_DEV
    piece = rows // groups
    enc = out_weight.shape[1]
    pieces = boundaries.shape[1] // piece
    vmem = pl.BlockSpec(memory_space=pltpu.VMEM)
    hbm = pl.BlockSpec(memory_space=pl.ANY)
    dma = pltpu.SemaphoreType.DMA
    operands = (
        step_decay,
        byte_input,
        b_proj,
        counts.reshape(1, 1),
        boundaries,
        c_proj,
        skip_gain.reshape(1, -1),
        out_weight,
        norm_gain.reshape(1, -1),
        qkv_weight,
    )
    result = pl.pallas_call(
        functools.partial(fused, seqs, groups),
        out_shape=jax.ShapeDtypeStruct((rows, width), OUT_WIRE),
        in_specs=[hbm] * len(operands),
        out_specs=vmem,
        scratch_shapes=[pltpu.VMEM(array.shape, array.dtype) for array in operands]
        + [
            pltpu.VMEM((seqs, lanes + EXTRA, state), STATE_WIRE),
            pltpu.VMEM((seqs, lanes + EXTRA, state), STATE_WIRE),
            pltpu.VMEM((seqs, lanes, state), STATE_WIRE),
            pltpu.VMEM((seqs, lanes, state), STATE_WIRE),
            pltpu.VMEM((pieces, piece, enc), PART_WIRE),
            pltpu.VMEM((2 * groups, piece, enc), PART_WIRE),
            pltpu.VMEM((groups, piece, enc), BF16),
            pltpu.VMEM((seqs, rows + rows // 2, 2 * lanes), BF16),
            pltpu.VMEM((seqs, rows + rows // 2, 2 * lanes), BF16),
            pltpu.VMEM((seqs, rows // 2, 2 * lanes), OUT_WIRE),
            pltpu.VMEM((seqs, rows // 2, 2 * lanes), OUT_WIRE),
            dma((len(operands),)),
            dma((2, seqs)),
            dma((2, seqs)),
            dma((2 * groups,)),
            dma((2 * groups,)),
            dma((2, groups)),
            dma((2, seqs)),
            dma((2, seqs)),
        ],
        compiler_params=pltpu.CompilerParams(collective_id=0, has_side_effects=True),
    )(*operands)
    return result.astype(F32)


def chosen(*args):
    byte_input, step_decay, slots = args[0], args[3], args[6].shape[1]
    heads = step_decay.shape[0]
    lanes = byte_input.shape[1] // heads
    seqs, groups = lax.axis_size("seq"), lax.axis_size("head")
    fits = seqs == heads and lanes == ATT_DIM and args[9].shape[2] == byte_input.shape[1]
    fits = fits and 2 * lanes == slots and args[1].shape[1] == slots and slots == 2 * ROWS_DEV
    fits = fits and seqs % 4 == 0 and groups % 2 == 0 and ROWS_DEV % (16 * groups) == 0
    fits = fits and byte_input.shape[0] % slots == 0
    return fused_body(*args) if fits else body(*args)


def solution(mesh):
    return jax.shard_map(
        chosen,
        mesh=mesh,
        in_specs=(
            P("seq", "head"),
            P("seq", None),
            P("seq", None),
            P("head", "seq"),
            P("head"),
            P("head", None),
            P("seq", None),
            P("seq"),
            P(),
            P(None, None, "head"),
        ),
        out_specs=P("seq", "head"),
        check_vma=False,
    )
```

profile of v0, /device:TPU:0, one launch (start us, length us, event | category | flops | bytes accessed | tf_op | source)
XLA Modules:
  0.0 40.0 jit_solution(13713088214175613985)
XLA Ops:
  0.7 37.8 %shard_map.100 = bf16[64,512]{1,0:T(8,128)(2,1)} custom-call(f32[8,384]{1,0:T(8,128)} %decay_hbm.1, f32[384,512]{1,0:T(8,128)} %x_hbm.1, f32[384,128]{1,0:T(8,128)} %b_hbm.1, s32[1,1]{1,0:T(1,128)} %bitcast.3.counts_hbm, s32[1,128]{1,0:T(1,128)} %bound_hbm.1, f32[384,128]{1,0:T(8,128)} %c_hbm.1, f32[1,8]{1,0:T(1,128)} %bitcast.5, ...), custom_call_target="tpu_custom_call" | custom-call | tf_op jit(solution)/shard_map/pallas_call | solution.py:588
  38.5 1.5 %convert_element_type.3 = f32[64,512]{1,0:T(8,128)} convert(bf16[64,512]{1,0:T(8,128)(2,1)} %shard_map.100) | non-fusion elementwise | flops 32768 | bytes 196608 | tf_op jit(solution)/shard_map/convert_element_type | solution.py:617
where the time goes:
time: 40.2 us; the launch traced here: 40 us
  Pallas kernels  37.8 us (94%)
  other arithmetic  1.5 us (4%)
  between operations  0.66 us (2%)
    pallas_call x1, Pallas kernels, fused_body(): pl.pallas_call(functools.partial(fused, seqs, groups), out_shape=jax.Shap...  37.8 us
    convert_element_type x1, other arithmetic, fused_body(): return result.astype(F32)  1.5 us

commit v1 on v0

--- a/solution.py
+++ b/solution.py
@@ -156,10 +156,7 @@
 
 F32 = jnp.float32
 BF16 = jnp.bfloat16
-STATE_WIRE = jnp.bfloat16
-PART_WIRE = jnp.bfloat16
-OUT_WIRE = jnp.bfloat16
-EXTRA = 16
+CHUNKS = 2
 
 
 def exact_dot(a, b, dims=((1,), (0,))):
@@ -205,6 +202,9 @@
     outw,
     gain_ref,
     qkvw,
+    x_both,
+    tag_send,
+    tag_recv,
     send_a,
     recv_a,
     send_b,
@@ -217,24 +217,33 @@
     send_o,
     recv_o,
     weight_sem,
-    a_sem,
-    b_sem,
+    tag_sem,
+    a_send,
+    a_recv,
+    b_send,
+    b_recv,
     p_send,
     p_recv,
     n_sem,
-    q_sem,
-    o_sem,
+    q_send,
+    q_recv,
+    o_send,
+    o_recv,
 ):
     me = lax.axis_index("seq")
     col = lax.axis_index("head")
     length, width = x_ref.shape
     heads = decay_ref.shape[0]
     lanes = width // heads
+    pair_width = 2 * lanes
+    pairs = heads // 2
     state = b_ref.shape[1]
     slots = bound_ref.shape[1]
     rows = out_ref.shape[0]
     piece = rows // groups
     half = rows // 2
+    lo = (seqs - pairs) // 2
+    is_owner = (me >= lo) & (me < lo + pairs)
 
     def shard_at(d):
         return lax.rem(me + d + seqs, seqs)
@@ -257,6 +266,10 @@
     def head_at(d):
         return lax.rem(col + d, groups)
 
+    chip = col // 2
+    partner = 2 * chip + 1 - lax.rem(col, 2)
+    other = 2 * (1 - chip)
+
     barrier = pltpu.get_barrier_semaphore()
     peers = [(shard_at(d), col) for d in range(1, seqs)]
     peers += [(me, head_at(d)) for d in range(1, groups)]
@@ -266,12 +279,12 @@
             barrier, inc=1, device_id=peer, device_id_type=pl.DeviceIdType.MESH
         )
 
-    def remote(src, dst, sems, k, source, peer):
+    def remote(src, dst, send_sem, recv_sem, peer):
         return pltpu.make_async_remote_copy(
             src_ref=src,
             dst_ref=dst,
-            send_sem=sems.at[0, k],
-            recv_sem=sems.at[1, source],
+            send_sem=send_sem,
+            recv_sem=recv_sem,
             device_id=peer,
             device_id_type=pl.DeviceIdType.MESH,
         )
@@ -299,37 +312,57 @@
     loads[0].wait()
     decay = decay_ref[...]
     upper = (iota((length, length), 0) <= iota((length, length), 1)).astype(F32)
+    logs = -exact_dot(decay, upper)
+    tail = jnp.exp(logs[:, length - 1 : length] - logs)
+    loads[3].wait()
+    tag_row = iota((heads, state), 1) == iota((heads, state), 0)
+    tags = jnp.where(tag_row, logs[:, length - 1 : length], 0.0)
+    tags = jnp.sum(tags, axis=0, keepdims=True)
+    number = jnp.broadcast_to(counts_ref[...].astype(F32), (1, state))
+    tag_send[...] = jnp.where(iota((1, state), 1) == heads, number, tags)
+    loads[1].wait()
+    loads[2].wait()
+    for load in loads[7:]:
+        load.start()
+    b_turned = b_ref[...].T
+    first_half = iota((state, pair_width), 1) < lanes
+    for pair in range(pairs):
+        x_high, x_low = halves(x_ref[:, pair * pair_width : (pair + 1) * pair_width])
+        both = jnp.concatenate([x_high, x_low], axis=1)
+        x_both[pair] = both
+        faded = [b_turned * tail[h : h + 1, :] for h in (2 * pair, 2 * pair + 1)]
+        f_high, f_low = halves(jnp.concatenate(faded, axis=0))
+        wide = fast_dot(f_high, both)
+        own = wide[:, :pair_width] + wide[:, pair_width:] + fast_dot(f_low, x_high)
+        send_a[pair] = jnp.where(first_half, own[:state], own[state:]).astype(BF16)
+    pl.semaphore_wait(barrier, len(peers))
+
+    def tag_copy(to, slot, source):
+        return remote(tag_send, tag_recv.at[slot], tag_sem.at[0, to], tag_sem.at[1, source], (to, col))
+
+    def a_copy(j, slot):
+        return remote(send_a.at[j], recv_a.at[slot], a_send.at[j], a_recv.at[slot], (lo + j, col))
+
+    for to in targets:
+        tag_copy(to, me, me).start()
+    for k in range(pairs):
+        j = jnp.where(near_end, pairs - 1 - k, k)
+
+        @pl.when(me != lo + j)
+        def _():
+            a_copy(j, me).start()
+
+    tag_recv[me] = tag_send[...]
+
+    @pl.when(is_owner)
+    def _():
+        recv_a[me] = send_a[me - lo]
+
     lower = (iota((length, length), 0) >= iota((length, length), 1)).astype(F32)
-    logs = -exact_dot(decay, upper)
     logs_t = -exact_dot(lower, decay, ((1,), (1,)))
     first = iota((heads, width), 0) * lanes
     channel = iota((heads, width), 1)
     spread = ((channel >= first) & (channel < first + lanes)).astype(F32)
-    tail_t = jnp.exp(logs_t[length - 1 : length, :] - logs_t)
-    loads[1].wait()
-    loads[2].wait()
-    loads[3].wait()
-    for load in loads[7:]:
-        load.start()
-    scaled = x_ref[...] * exact_dot(tail_t, spread)
-    own = exact_dot(scaled, b_ref[...], ((0,), (0,)))
-    number = jnp.broadcast_to(counts_ref[...].astype(F32), (EXTRA, state))
-    extra_row = iota((EXTRA, state), 0)
-    for h in range(heads):
-        send_a[h, :lanes, :] = own[h * lanes : (h + 1) * lanes, :].astype(send_a.dtype)
-        last = jnp.broadcast_to(logs[h : h + 1, length - 1 : length], (EXTRA, state))
-        last_high, rest = halves(last)
-        rest = last - last_high.astype(F32)
-        last_mid, last_low = halves(rest)
-        extra = jnp.where(extra_row == 1, last_mid.astype(F32), last_high.astype(F32))
-        extra = jnp.where(extra_row == 2, last_low.astype(F32), extra)
-        extra = jnp.where(extra_row == 3, number, extra)
-        send_a[h, lanes:, :] = extra.astype(send_a.dtype)
-    pl.semaphore_wait(barrier, len(peers))
-    for to in targets:
-        remote(send_a.at[to], recv_a.at[me], a_sem, to, me, (to, col)).start()
-    recv_a[me] = send_a[me]
-
     for load in loads[4:7]:
         load.wait()
     marks = jnp.broadcast_to(bound_ref[...].astype(F32), (slots, slots)).T
@@ -342,73 +375,88 @@
     logs_sel = exact_dot(onehot, logs_t)
     affinity = exact_dot(c_rows, b_ref[...], ((1,), (1,)))
     inside = []
-    first_lane = iota((slots, 2 * lanes), 1) < lanes
-    for pair in range(heads // 2):
-        x_high, x_low = halves(x_ref[:, pair * 2 * lanes : (pair + 1) * 2 * lanes])
-        x_both = jnp.concatenate([x_high, x_low], axis=1)
+    first_lane = iota((slots, pair_width), 1) < lanes
+    for pair in range(pairs):
+        both = x_both[pair]
         parts = []
         for h in (2 * pair, 2 * pair + 1):
             gap = logs_sel[:, h : h + 1] - logs[h : h + 1, :]
             weights = jnp.where(seen, jnp.exp(jnp.where(seen, gap, 0.0)), 0.0) * affinity
             weights = weights + jnp.where(hit, skip_ref[:, h : h + 1], 0.0)
             w_high, w_low = halves(weights)
-            wide = fast_dot(w_high, x_both)
+            wide = fast_dot(w_high, both)
             parts.append(
-                wide[:, : 2 * lanes] + wide[:, 2 * lanes :] + fast_dot(w_low, x_high)
+                wide[:, :pair_width] + wide[:, pair_width:] + fast_dot(w_low, both[:, :pair_width])
             )
         inside.append(jnp.where(first_lane, parts[0], parts[1]))
     inside = jnp.concatenate(inside, axis=1)
     enter_scale = exact_dot(jnp.exp(logs_sel), spread)
+    c_high, c_low = halves(c_rows)
 
     for d in range(1, seqs):
         source = shard_at(-d)
-        copy = remote(send_a.at[shard_at(d)], recv_a.at[source], a_sem, source, source, (source, col))
-        copy.wait_recv()
-    running = jnp.zeros((lanes, state), F32)
-    for s in range(seqs):
-        send_b[s] = running.astype(send_b.dtype)
-        if s < seqs - 1:
-            tags = recv_a[s, lanes:, :].astype(F32)
-            kept = jnp.exp((tags[0:1] + tags[1:2]) + tags[2:3])
-            running = kept * running + recv_a[s, :lanes, :].astype(F32)
-    for to in targets:
-        remote(send_b.at[to], recv_b.at[me], b_sem, to, me, (to, col)).start()
-    recv_b[me] = send_b[me]
-
-    start = jnp.zeros((1, state), F32)
-    for s in range(seqs):
-        start = start + jnp.where(s < me, recv_a[s, lanes:, :].astype(F32)[3:4], 0.0)
+        tag_copy(shard_at(d), source, source).wait_recv()
+    all_tags = tag_recv[...].reshape(seqs, state)
+    tag_lane = iota((seqs, state), 1)
+
+    def b_copy(s, j):
+        return remote(send_b.at[s], recv_b.at[j], b_send.at[s], b_recv.at[j], (s, col))
+
+    @pl.when(is_owner)
+    def _():
+        mine = me - lo
+        even = jnp.sum(jnp.where(tag_lane == 2 * mine, all_tags, 0.0), axis=1, keepdims=True)
+        odd = jnp.sum(jnp.where(tag_lane == 2 * mine + 1, all_tags, 0.0), axis=1, keepdims=True)
+        kept = jnp.exp(jnp.where(iota((seqs, pair_width), 1) < lanes, even, odd))
+        running = jnp.zeros((state, pair_width), F32)
+        for s in range(seqs):
+            send_b[s] = running.astype(BF16)
+
+            @pl.when(me != s)
+            def _():
+                b_copy(s, mine).start()
+
+            if s < seqs - 1:
+
+                @pl.when(me != s)
+                def _():
+                    a_copy(mine, s).wait_recv()
+
+                running = kept[s : s + 1] * running + recv_a[s].astype(F32)
+
+        @pl.when(me != seqs - 1)
+        def _():
+            a_copy(mine, seqs - 1).wait_recv()
+
+        recv_b[mine] = send_b[me]
+
+    earlier = (iota((seqs, state), 0) < me) & (tag_lane == heads)
+    start = jnp.sum(jnp.where(earlier, all_tags, 0.0), axis=(0, 1), keepdims=True)
     offset = start - (me * rows - half).astype(F32)
     slot = iota((slots, slots), 1).astype(F32)
-    mine = jnp.broadcast_to(counts_ref[...].astype(F32), (slots, slots))
-    shift = (slot == iota((slots, slots), 0).astype(F32) - offset) & (slot < mine)
+    count = jnp.broadcast_to(counts_ref[...].astype(F32), (slots, slots))
+    shift = (slot == iota((slots, slots), 0).astype(F32) - offset) & (slot < count)
     shift = shift.astype(BF16)
 
-    for d in range(1, seqs):
-        source = shard_at(-d)
-        remote(send_b.at[shard_at(d)], recv_b.at[source], b_sem, source, source, (source, col)).wait_recv()
-    entering = recv_b[...].reshape(heads * lanes, state)
-    c_high, c_low = halves(c_rows)
-    last_dims = ((1,), (1,))
-    carried = fast_dot(c_high, entering, last_dims) + fast_dot(c_low, entering, last_dims)
+    for j in range(pairs):
+
+        @pl.when(me != lo + j)
+        def _():
+            b_copy(me, j).wait_recv()
+
+    entering = jnp.concatenate([recv_b[j] for j in range(pairs)], axis=1)
+    carried = fast_dot(c_high, entering) + fast_dot(c_low, entering)
     y = (inside + enter_scale * carried).astype(BF16)
     window = fast_dot(shift, y).astype(BF16)
     loads[7].wait()
     partial = fast_dot(window, outw[...])
     pieces = slots // piece
     for i in range(pieces):
-        send_p[i] = partial[i * piece : (i + 1) * piece, :].astype(send_p.dtype)
+        send_p[i] = partial[i * piece : (i + 1) * piece, :].astype(BF16)
     outer = (pieces - groups) // 2
 
     def project(src, slot, k, peer):
-        return pltpu.make_async_remote_copy(
-            src_ref=send_p.at[src],
-            dst_ref=recv_p.at[slot],
-            send_sem=p_send.at[k],
-            recv_sem=p_recv.at[slot],
-            device_id=peer,
-            device_id_type=pl.DeviceIdType.MESH,
-        )
+        return remote(send_p.at[src], recv_p.at[slot], p_send.at[k], p_recv.at[slot], peer)
 
     below_sent = [project(i, groups + col, i, (shard_at(-1), groups - outer + i)) for i in range(outer)]
     above_sent = [
@@ -455,75 +503,130 @@
     square = jnp.mean(mixed * mixed, axis=-1, keepdims=True)
     normed = (mixed * lax.rsqrt(square + 1e-05) * gain_ref[...]).astype(BF16)
     recv_n[col] = normed
-    sent_n = []
-    for d in range(1, groups):
-        to = head_at(d)
-        sent_n.append(remote(recv_n.at[col], recv_n.at[col], n_sem, to, col, (me, to)))
-        sent_n[-1].start()
-    for d in range(1, groups):
-        source = head_at(groups - d)
-        remote(recv_n.at[col], recv_n.at[source], n_sem, source, source, (me, source)).wait_recv()
-    normed = recv_n[...].reshape(rows, -1)
+
+    def n_copy(to, source):
+        return remote(recv_n.at[col], recv_n.at[source], n_sem.at[0, to], n_sem.at[1, source], (me, to))
+
+    sent_n = [n_copy(to, col) for to in (other, other + 1, partner)]
+    for copy in sent_n:
+        copy.start()
     loads[9].wait()
-    query, key, value = [
-        fast_dot(normed, qkvw[i]).astype(BF16).astype(F32) for i in range(3)
-    ]
-    pair_width = 2 * lanes
-    left = iota((rows, pair_width), 1) < lanes
-    left_half = left[:half]
+    near = rows // CHUNKS
+    quarter = near // 2
+    left = iota((near, pair_width), 1) < lanes
+    left_quarter = left[:quarter]
 
     def turned(a):
         return pltpu.roll(a, lanes, 1)
 
-    for pair in range(heads // 2):
-        at = slice(pair * pair_width, (pair + 1) * pair_width)
-        q, k, v = query[:, at], key[:, at], value[:, at]
-        send_q[2 * pair, :rows, :] = jnp.where(left, q, turned(k)).astype(BF16)
-        send_q[2 * pair + 1, :rows, :] = jnp.where(left, turned(q), k).astype(BF16)
-        above, below = v[:half], v[half:]
-        send_q[2 * pair, rows:, :] = jnp.where(left_half, above, turned(below)).astype(BF16)
-        send_q[2 * pair + 1, rows:, :] = jnp.where(
-            left_half, turned(above), below
-        ).astype(BF16)
-    for to in targets:
-        remote(send_q.at[to], recv_q.at[me], q_sem, to, me, (to, col)).start()
+    def q_copy(to, slot, part):
+        return remote(
+            send_q.at[to, part],
+            recv_q.at[slot, part],
+            q_send.at[part, to],
+            q_recv.at[part, slot],
+            (to, col),
+        )
+
+    for sources, part in (((partner,), chip), ((other, other + 1), 1 - chip)):
+        for source in sources:
+            n_copy(source, source).wait_recv()
+        block = recv_n[pl.ds(2 * part, 2)].reshape(near, -1)
+        query, key, value = [
+            fast_dot(block, qkvw[i]).astype(BF16).astype(F32) for i in range(3)
+        ]
+        for pair in range(pairs):
+            at = slice(pair * pair_width, (pair + 1) * pair_width)
+            q, k, v = query[:, at], key[:, at], value[:, at]
+            above, below = v[:quarter], v[quarter:]
+            send_q[2 * pair, part, :near, :] = jnp.where(left, q, turned(k)).astype(BF16)
+            send_q[2 * pair + 1, part, :near, :] = jnp.where(left, turned(q), k).astype(BF16)
+            send_q[2 * pair, part, near:, :] = jnp.where(left_quarter, above, turned(below)).astype(
+                BF16
+            )
+            send_q[2 * pair + 1, part, near:, :] = jnp.where(
+                left_quarter, turned(above), below
+            ).astype(BF16)
+        for to in targets:
+            q_copy(to, me, part).start()
     recv_q[me] = send_q[me]
-    for d in range(1, seqs):
-        source = shard_at(-d)
-        remote(send_q.at[shard_at(d)], recv_q.at[source], q_sem, source, source, (source, col)).wait_recv()
-    coarse = seqs * rows
-    both = recv_q[:, :rows, :].reshape(coarse, pair_width)
-    wide = both.astype(F32)
-    left_all = iota((coarse, pair_width), 1) < lanes
+
+    def unpack(ref, at):
+        both = ref[at, :, :near, :].reshape(rows, pair_width).astype(F32)
+        packed = ref[at, :, near:, :].astype(F32)
+        values = []
+        for part in range(CHUNKS):
+            values += [packed[part], turned(packed[part])]
+        return both, values
+
+    def attend(queries, keys, values, first_row):
+        scores = fast_dot(queries, keys, ((1,), (1,))) * (lanes ** (-0.5))
+        allowed = first_row + iota(scores.shape, 0) >= iota(scores.shape, 1)
+        scores = jnp.where(allowed, scores, -1e30)
+        highest = jnp.max(scores, axis=-1, keepdims=True)
+        exps = jnp.where(allowed, jnp.exp(scores - highest), 0.0)
+        total = jnp.sum(exps, axis=-1, keepdims=True)
+        return fast_dot(exps.astype(BF16), values) / total
+
+    @pl.when(me == 0)
+    def _():
+        left_rows = iota((rows, pair_width), 1) < lanes
+        for pair in range(pairs):
+            results = []
+            for h in (2 * pair, 2 * pair + 1):
+                both, values = unpack(send_q, h)
+                queries = jnp.where(left_rows, both, 0.0).astype(BF16)
+                keys = turned(both).astype(BF16)
+                values = jnp.concatenate(values, axis=0).astype(BF16)
+                results.append(attend(queries, keys, values, 0))
+            out_ref[:, pair * pair_width : (pair + 1) * pair_width] = jnp.where(
+                left_rows, results[0], turned(results[1])
+            ).astype(out_ref.dtype)
+
+    for part in (chip, 1 - chip):
+        for d in range(1, seqs):
+            source = shard_at(-d)
+            q_copy(shard_at(d), source, part).wait_recv()
+    wide, values = [], []
+    for s in range(seqs):
+        both, some = unpack(recv_q, s)
+        wide.append(both)
+        values += some
+    wide = jnp.concatenate(wide, axis=0)
+    values = jnp.concatenate(values, axis=0).astype(BF16)
+    left_all = iota(wide.shape, 1) < lanes
     queries = jnp.where(left_all, wide, 0.0).astype(BF16)
     keys = turned(wide).astype(BF16)
-    values = []
-    for s in range(seqs):
-        packed = recv_q[s, rows:, :].astype(F32)
-        values += [packed, turned(packed)]
-    values = jnp.concatenate(values, axis=0).astype(BF16)
-    scores = fast_dot(queries, keys, ((1,), (1,))) * (lanes ** (-0.5))
-    allowed = iota((coarse, coarse), 0) >= iota((coarse, coarse), 1)
-    scores = jnp.where(allowed, scores, -1e30)
-    highest = jnp.max(scores, axis=-1, keepdims=True)
-    exps = jnp.where(allowed, jnp.exp(scores - highest), 0.0)
-    total = jnp.sum(exps, axis=-1, keepdims=True)
-    result = fast_dot(exps.astype(BF16), values) / total
-    for s in range(seqs):
-        above = result[s * rows : s * rows + half]
-        below = result[s * rows + half : (s + 1) * rows]
-        send_o[s] = jnp.where(left_half, above, turned(below)).astype(send_o.dtype)
-    for to in targets:
-        remote(send_o.at[to], recv_o.at[me], o_sem, to, me, (to, col)).start()
-    recv_o[me] = send_o[me]
-    for d in range(1, seqs):
-        source = shard_at(-d)
-        remote(send_o.at[shard_at(d)], recv_o.at[source], o_sem, source, source, (source, col)).wait_recv()
-    for pair in range(heads // 2):
-        at = slice(pair * pair_width, (pair + 1) * pair_width)
-        even, odd = recv_o[2 * pair].astype(F32), recv_o[2 * pair + 1].astype(F32)
-        out_ref[:half, at] = jnp.where(left_half, even, turned(odd)).astype(OUT_WIRE)
-        out_ref[half:, at] = jnp.where(left_half, turned(even), odd).astype(OUT_WIRE)
+    left_half = iota((half, pair_width), 1) < lanes
+
+    def o_copy(s, slot):
+        return remote(send_o.at[s], recv_o.at[slot], o_send.at[s], o_recv.at[slot], (s, col))
+
+    span = 2 * rows
+    for k in range(seqs // 2):
+        end = (k + 1) * span
+        result = attend(queries[k * span : end], keys[:end], values[:end], k * span)
+        for s in (2 * k, 2 * k + 1):
+            if s == 0:
+                continue
+            at = (s - 2 * k) * rows
+            above, below = result[at : at + half], result[at + half : at + rows]
+            send_o[s] = jnp.where(left_half, above, turned(below)).astype(BF16)
+
+            @pl.when(me != s)
+            def _():
+                o_copy(s, me).start()
+
+    @pl.when(me > 0)
+    def _():
+        recv_o[me] = send_o[me]
+        for d in range(1, seqs):
+            o_copy(me, shard_at(-d)).wait_recv()
+        for pair in range(pairs):
+            at = slice(pair * pair_width, (pair + 1) * pair_width)
+            even, odd = recv_o[2 * pair].astype(F32), recv_o[2 * pair + 1].astype(F32)
+            out_ref[:half, at] = jnp.where(left_half, even, turned(odd)).astype(out_ref.dtype)
+            out_ref[half:, at] = jnp.where(left_half, turned(even), odd).astype(out_ref.dtype)
 
     for copy in sent + sent_n:
         copy.wait_send()
@@ -538,15 +641,28 @@
         for copy in above_sent:
             copy.wait_send()
 
-    for sems, send, recv in (
-        (a_sem, send_a, recv_a),
-        (b_sem, send_b, recv_b),
-        (q_sem, send_q, recv_q),
-        (o_sem, send_o, recv_o),
-    ):
-        for d in range(1, seqs):
-            to = shard_at(d)
-            remote(send.at[to], recv.at[me], sems, to, me, (to, col)).wait_send()
+    for j in range(pairs):
+
+        @pl.when(me != lo + j)
+        def _():
+            a_copy(j, me).wait_send()
+
+    for to in targets:
+        tag_copy(to, me, me).wait_send()
+        for part in range(CHUNKS):
+            q_copy(to, me, part).wait_send()
+
+    for s in range(seqs):
+
+        @pl.when(is_owner & (me != s))
+        def _():
+            b_copy(s, me - lo).wait_send()
+
+        if s > 0:
+
+            @pl.when(me != s)
+            def _():
+                o_copy(s, me).wait_send()
 
 
 def fused_body(
@@ -563,13 +679,15 @@
 ):
     seqs, groups = lax.axis_size("seq"), lax.axis_size("head")
     heads = step_decay.shape[0]
-    width = byte_input.shape[1]
+    length, width = byte_input.shape
     lanes = width // heads
+    pairs = heads // 2
     state = b_proj.shape[1]
     rows = ROWS_DEV
     piece = rows // groups
     enc = out_weight.shape[1]
     pieces = boundaries.shape[1] // piece
+    packed = rows // CHUNKS + rows // (2 * CHUNKS)
     vmem = pl.BlockSpec(memory_space=pltpu.VMEM)
     hbm = pl.BlockSpec(memory_space=pl.ANY)
     dma = pltpu.SemaphoreType.DMA
@@ -587,30 +705,38 @@
     )
     result = pl.pallas_call(
         functools.partial(fused, seqs, groups),
-        out_shape=jax.ShapeDtypeStruct((rows, width), OUT_WIRE),
+        out_shape=jax.ShapeDtypeStruct((rows, width), BF16),
         in_specs=[hbm] * len(operands),
         out_specs=vmem,
         scratch_shapes=[pltpu.VMEM(array.shape, array.dtype) for array in operands]
         + [
-            pltpu.VMEM((seqs, lanes + EXTRA, state), STATE_WIRE),
-            pltpu.VMEM((seqs, lanes + EXTRA, state), STATE_WIRE),
-            pltpu.VMEM((seqs, lanes, state), STATE_WIRE),
-            pltpu.VMEM((seqs, lanes, state), STATE_WIRE),
-            pltpu.VMEM((pieces, piece, enc), PART_WIRE),
-            pltpu.VMEM((2 * groups, piece, enc), PART_WIRE),
+            pltpu.VMEM((pairs, length, 4 * lanes), BF16),
+            pltpu.VMEM((1, state), F32),
+            pltpu.VMEM((seqs, 1, state), F32),
+            pltpu.VMEM((pairs, state, 2 * lanes), BF16),
+            pltpu.VMEM((seqs, state, 2 * lanes), BF16),
+            pltpu.VMEM((seqs, state, 2 * lanes), BF16),
+            pltpu.VMEM((pairs, state, 2 * lanes), BF16),
+            pltpu.VMEM((pieces, piece, enc), BF16),
+            pltpu.VMEM((2 * groups, piece, enc), BF16),
             pltpu.VMEM((groups, piece, enc), BF16),
-            pltpu.VMEM((seqs, rows + rows // 2, 2 * lanes), BF16),
-            pltpu.VMEM((seqs, rows + rows // 2, 2 * lanes), BF16),
-            pltpu.VMEM((seqs, rows // 2, 2 * lanes), OUT_WIRE),
-            pltpu.VMEM((seqs, rows // 2, 2 * lanes), OUT_WIRE),
+            pltpu.VMEM((seqs, CHUNKS, packed, 2 * lanes), BF16),
+            pltpu.VMEM((seqs, CHUNKS, packed, 2 * lanes), BF16),
+            pltpu.VMEM((seqs, rows // 2, 2 * lanes), BF16),
+            pltpu.VMEM((seqs, rows // 2, 2 * lanes), BF16),
             dma((len(operands),)),
             dma((2, seqs)),
-            dma((2, seqs)),
+            dma((pairs,)),
+            dma((seqs,)),
+            dma((seqs,)),
+            dma((pairs,)),
             dma((2 * groups,)),
             dma((2 * groups,)),
             dma((2, groups)),
-            dma((2, seqs)),
-            dma((2, seqs)),
+            dma((CHUNKS, seqs)),
+            dma((CHUNKS, seqs)),
+            dma((seqs,)),
+            dma((seqs,)),
         ],
         compiler_params=pltpu.CompilerParams(collective_id=0, has_side_effects=True),
     )(*operands)
@@ -624,7 +750,7 @@
     seqs, groups = lax.axis_size("seq"), lax.axis_size("head")
     fits = seqs == heads and lanes == ATT_DIM and args[9].shape[2] == byte_input.shape[1]
     fits = fits and 2 * lanes == slots and args[1].shape[1] == slots and slots == 2 * ROWS_DEV
-    fits = fits and seqs % 4 == 0 and groups % 2 == 0 and ROWS_DEV % (16 * groups) == 0
+    fits = fits and seqs % 4 == 0 and groups == 2 * CHUNKS and ROWS_DEV % (16 * groups) == 0
     fits = fits and byte_input.shape[0] % slots == 0
     return fused_body(*args) if fits else body(*args)
 

time: 40.2 us -> 36.6 us (0.910)
  the two profiles are of different devices: /device:TPU:0 before, /device:TPU:24 now
where the time goes in v1:
time: 36.6 us; the launch traced here: 36.1 us
  Pallas kernels  33.9 us (93%)
  other arithmetic  1.5 us (4%)
  between operations  0.66 us (2%)
    pallas_call x1, Pallas kernels, fused_body(): pl.pallas_call(functools.partial(fused, seqs, groups), out_shape=jax.Shap...  33.9 us
    convert_element_type x1, other arithmetic, fused_body(): return result.astype(F32)  1.5 us

profile of v1, /device:TPU:24, one launch (start us, length us, event | category | flops | bytes accessed | tf_op | source)
XLA Modules:
  0.0 36.1 jit_solution(11016329766914640625)
XLA Ops:
  0.7 33.9 %shard_map.100 = bf16[64,512]{1,0:T(8,128)(2,1)} custom-call(f32[8,384]{1,0:T(8,128)} %decay_hbm.1, f32[384,512]{1,0:T(8,128)} %x_hbm.1, f32[384,128]{1,0:T(8,128)} %b_hbm.1, s32[1,1]{1,0:T(1,128)} %bitcast.3.counts_hbm, s32[1,128]{1,0:T(1,128)} %bound_hbm.1, f32[384,128]{1,0:T(8,128)} %c_hbm.1, f32[1,8]{1,0:T(1,128)} %bitcast.5, ...), custom_call_target="tpu_custom_call" | custom-call | tf_op jit(solution)/shard_map/pallas_call | solution.py:706
  34.6 1.5 %convert_element_type.3 = f32[64,512]{1,0:T(8,128)} convert(bf16[64,512]{1,0:T(8,128)(2,1)} %shard_map.100) | non-fusion elementwise | flops 32768 | bytes 196608 | tf_op jit(solution)/shard_map/convert_element_type | solution.py:743

commit v2 on v1

--- a/solution.py
+++ b/solution.py
@@ -215,7 +215,7 @@
     send_q,
     recv_q,
     send_o,
-    recv_o,
+    first_out,
     weight_sem,
     tag_sem,
     a_send,
@@ -229,6 +229,7 @@
     q_recv,
     o_send,
     o_recv,
+    out_sem,
 ):
     me = lax.axis_index("seq")
     col = lax.axis_index("head")
@@ -512,121 +513,93 @@
         copy.start()
     loads[9].wait()
     near = rows // CHUNKS
-    quarter = near // 2
-    left = iota((near, pair_width), 1) < lanes
-    left_quarter = left[:quarter]
-
-    def turned(a):
-        return pltpu.roll(a, lanes, 1)
-
-    def q_copy(to, slot, part):
+
+    def q_copy(j, slot, part):
         return remote(
-            send_q.at[to, part],
+            send_q.at[j, part],
             recv_q.at[slot, part],
-            q_send.at[part, to],
+            q_send.at[part, j],
             q_recv.at[part, slot],
-            (to, col),
+            (lo + j, col),
         )
 
     for sources, part in (((partner,), chip), ((other, other + 1), 1 - chip)):
         for source in sources:
             n_copy(source, source).wait_recv()
         block = recv_n[pl.ds(2 * part, 2)].reshape(near, -1)
-        query, key, value = [
-            fast_dot(block, qkvw[i]).astype(BF16).astype(F32) for i in range(3)
-        ]
+        for i in range(3):
+            product = fast_dot(block, qkvw[i]).astype(BF16)
+            for pair in range(pairs):
+                send_q[pair, part, i] = product[:, pair * pair_width : (pair + 1) * pair_width]
+        for k in range(pairs):
+            j = jnp.where(near_end, pairs - 1 - k, k)
+
+            @pl.when(me != lo + j)
+            def _():
+                q_copy(j, me, part).start()
+
+    def attend(queries, keys, values, first_row):
+        left = iota(queries.shape, 1) < lanes
+        results = []
+        for keep in (left, jnp.logical_not(left)):
+            masked = jnp.where(keep, queries.astype(F32), 0.0).astype(BF16)
+            scores = fast_dot(masked, keys, ((1,), (1,))) * (lanes ** (-0.5))
+            allowed = first_row + iota(scores.shape, 0) >= iota(scores.shape, 1)
+            scores = jnp.where(allowed, scores, -1e30)
+            highest = jnp.max(scores, axis=-1, keepdims=True)
+            exps = jnp.where(allowed, jnp.exp(scores - highest), 0.0)
+            total = jnp.sum(exps, axis=-1, keepdims=True)
+            results.append(fast_dot(exps.astype(BF16), values) / total)
+        return jnp.where(left, results[0], results[1]).astype(BF16)
+
+    @pl.when(me == 0)
+    def _():
         for pair in range(pairs):
-            at = slice(pair * pair_width, (pair + 1) * pair_width)
-            q, k, v = query[:, at], key[:, at], value[:, at]
-            above, below = v[:quarter], v[quarter:]
-            send_q[2 * pair, part, :near, :] = jnp.where(left, q, turned(k)).astype(BF16)
-            send_q[2 * pair + 1, part, :near, :] = jnp.where(left, turned(q), k).astype(BF16)
-            send_q[2 * pair, part, near:, :] = jnp.where(left_quarter, above, turned(below)).astype(
-                BF16
-            )
-            send_q[2 * pair + 1, part, near:, :] = jnp.where(
-                left_quarter, turned(above), below
-            ).astype(BF16)
-        for to in targets:
-            q_copy(to, me, part).start()
-    recv_q[me] = send_q[me]
-
-    def unpack(ref, at):
-        both = ref[at, :, :near, :].reshape(rows, pair_width).astype(F32)
-        packed = ref[at, :, near:, :].astype(F32)
-        values = []
-        for part in range(CHUNKS):
-            values += [packed[part], turned(packed[part])]
-        return both, values
-
-    def attend(queries, keys, values, first_row):
-        scores = fast_dot(queries, keys, ((1,), (1,))) * (lanes ** (-0.5))
-        allowed = first_row + iota(scores.shape, 0) >= iota(scores.shape, 1)
-        scores = jnp.where(allowed, scores, -1e30)
-        highest = jnp.max(scores, axis=-1, keepdims=True)
-        exps = jnp.where(allowed, jnp.exp(scores - highest), 0.0)
-        total = jnp.sum(exps, axis=-1, keepdims=True)
-        return fast_dot(exps.astype(BF16), values) / total
+            q, k, v = [send_q[pair, :, i].reshape(rows, pair_width) for i in range(3)]
+            first_out[:, pair * pair_width : (pair + 1) * pair_width] = attend(q, k, v, 0)
+        pltpu.make_async_copy(first_out, out_ref, out_sem).start()
+
+    def o_copy(s, j):
+        place = pl.ds(pl.multiple_of(j * pair_width, pair_width), pair_width)
+        return remote(send_o.at[s], out_ref.at[:, place], o_send.at[s], o_recv.at[j], (s, col))
+
+    def o_keep(j):
+        place = pl.ds(pl.multiple_of(j * pair_width, pair_width), pair_width)
+        return pltpu.make_async_copy(send_o.at[me], out_ref.at[:, place], out_sem)
+
+    @pl.when(is_owner)
+    def _():
+        mine = me - lo
+        recv_q[me] = send_q[mine]
+        for part in (chip, 1 - chip):
+            for d in range(1, seqs):
+                q_copy(mine, shard_at(-d), part).wait_recv()
+        q, k, v = [recv_q[:, :, i].reshape(seqs * rows, pair_width) for i in range(3)]
+        span = 2 * rows
+        for n in range(seqs // 2):
+            end = (n + 1) * span
+            result = attend(q[n * span : end], k[:end], v[:end], n * span)
+            for s in (2 * n, 2 * n + 1):
+                if s == 0:
+                    continue
+                send_o[s] = result[(s - 2 * n) * rows : (s - 2 * n + 1) * rows]
+
+                @pl.when(me != s)
+                def _():
+                    o_copy(s, mine).start()
+
+        o_keep(mine).start()
+        o_keep(mine).wait()
 
     @pl.when(me == 0)
     def _():
-        left_rows = iota((rows, pair_width), 1) < lanes
-        for pair in range(pairs):
-            results = []
-            for h in (2 * pair, 2 * pair + 1):
-                both, values = unpack(send_q, h)
-                queries = jnp.where(left_rows, both, 0.0).astype(BF16)
-                keys = turned(both).astype(BF16)
-                values = jnp.concatenate(values, axis=0).astype(BF16)
-                results.append(attend(queries, keys, values, 0))
-            out_ref[:, pair * pair_width : (pair + 1) * pair_width] = jnp.where(
-                left_rows, results[0], turned(results[1])
-            ).astype(out_ref.dtype)
-
-    for part in (chip, 1 - chip):
-        for d in range(1, seqs):
-            source = shard_at(-d)
-            q_copy(shard_at(d), source, part).wait_recv()
-    wide, values = [], []
-    for s in range(seqs):
-        both, some = unpack(recv_q, s)
-        wide.append(both)
-        values += some
-    wide = jnp.concatenate(wide, axis=0)
-    values = jnp.concatenate(values, axis=0).astype(BF16)
-    left_all = iota(wide.shape, 1) < lanes
-    queries = jnp.where(left_all, wide, 0.0).astype(BF16)
-    keys = turned(wide).astype(BF16)
-    left_half = iota((half, pair_width), 1) < lanes
-
-    def o_copy(s, slot):
-        return remote(send_o.at[s], recv_o.at[slot], o_send.at[s], o_recv.at[slot], (s, col))
-
-    span = 2 * rows
-    for k in range(seqs // 2):
-        end = (k + 1) * span
-        result = attend(queries[k * span : end], keys[:end], values[:end], k * span)
-        for s in (2 * k, 2 * k + 1):
-            if s == 0:
-                continue
-            at = (s - 2 * k) * rows
-            above, below = result[at : at + half], result[at + half : at + rows]
-            send_o[s] = jnp.where(left_half, above, turned(below)).astype(BF16)
-
-            @pl.when(me != s)
-            def _():
-                o_copy(s, me).start()
-
-    @pl.when(me > 0)
-    def _():
-        recv_o[me] = send_o[me]
-        for d in range(1, seqs):
-            o_copy(me, shard_at(-d)).wait_recv()
-        for pair in range(pairs):
-            at = slice(pair * pair_width, (pair + 1) * pair_width)
-            even, odd = recv_o[2 * pair].astype(F32), recv_o[2 * pair + 1].astype(F32)
-            out_ref[:half, at] = jnp.where(left_half, even, turned(odd)).astype(out_ref.dtype)
-            out_ref[half:, at] = jnp.where(left_half, turned(even), odd).astype(out_ref.dtype)
+        pltpu.make_async_copy(first_out, out_ref, out_sem).wait()
+
+    for j in range(pairs):
+
+        @pl.when((me > 0) & (me != lo + j))
+        def _():
+            o_copy(me, j).wait_recv()
 
     for copy in sent + sent_n:
         copy.wait_send()
@@ -646,11 +619,11 @@
         @pl.when(me != lo + j)
         def _():
             a_copy(j, me).wait_send()
+            for part in range(CHUNKS):
+                q_copy(j, me, part).wait_send()
 
     for to in targets:
         tag_copy(to, me, me).wait_send()
-        for part in range(CHUNKS):
-            q_copy(to, me, part).wait_send()
 
     for s in range(seqs):
 
@@ -660,9 +633,9 @@
 
         if s > 0:
 
-            @pl.when(me != s)
+            @pl.when(is_owner & (me != s))
             def _():
-                o_copy(s, me).wait_send()
+                o_copy(s, me - lo).wait_send()
 
 
 def fused_body(
@@ -687,8 +660,6 @@
     piece = rows // groups
     enc = out_weight.shape[1]
     pieces = boundaries.shape[1] // piece
-    packed = rows // CHUNKS + rows // (2 * CHUNKS)
-    vmem = pl.BlockSpec(memory_space=pltpu.VMEM)
     hbm = pl.BlockSpec(memory_space=pl.ANY)
     dma = pltpu.SemaphoreType.DMA
     operands = (
@@ -707,7 +678,7 @@
         functools.partial(fused, seqs, groups),
         out_shape=jax.ShapeDtypeStruct((rows, width), BF16),
         in_specs=[hbm] * len(operands),
-        out_specs=vmem,
+        out_specs=hbm,
         scratch_shapes=[pltpu.VMEM(array.shape, array.dtype) for array in operands]
         + [
             pltpu.VMEM((pairs, length, 4 * lanes), BF16),
@@ -720,10 +691,10 @@
             pltpu.VMEM((pieces, piece, enc), BF16),
             pltpu.VMEM((2 * groups, piece, enc), BF16),
             pltpu.VMEM((groups, piece, enc), BF16),
-            pltpu.VMEM((seqs, CHUNKS, packed, 2 * lanes), BF16),
-            pltpu.VMEM((seqs, CHUNKS, packed, 2 * lanes), BF16),
-            pltpu.VMEM((seqs, rows // 2, 2 * lanes), BF16),
-            pltpu.VMEM((seqs, rows // 2, 2 * lanes), BF16),
+            pltpu.VMEM((pairs, CHUNKS, 3, rows // CHUNKS, 2 * lanes), BF16),
+            pltpu.VMEM((seqs, CHUNKS, 3, rows // CHUNKS, 2 * lanes), BF16),
+            pltpu.VMEM((seqs, rows, 2 * lanes), BF16),
+            pltpu.VMEM((rows, width), BF16),
             dma((len(operands),)),
             dma((2, seqs)),
             dma((pairs,)),
@@ -733,10 +704,11 @@
             dma((2 * groups,)),
             dma((2 * groups,)),
             dma((2, groups)),
-            dma((CHUNKS, seqs)),
+            dma((CHUNKS, pairs)),
             dma((CHUNKS, seqs)),
             dma((seqs,)),
-            dma((seqs,)),
+            dma((pairs,)),
+            dma,
         ],
         compiler_params=pltpu.CompilerParams(collective_id=0, has_side_effects=True),
     )(*operands)

time: 36.6 us -> 36 us (0.984)
  no operation moved by 1% of the time
where the time goes in v2:
time: 36 us; the launch traced here: 35.8 us
  Pallas kernels  33.7 us (94%)
  other arithmetic  1.5 us (4%)
  between operations  0.66 us (2%)
    pallas_call x1, Pallas kernels, fused_body(): pl.pallas_call(functools.partial(fused, seqs, groups), out_shape=jax.Shap...  33.7 us
    convert_element_type x1, other arithmetic, fused_body(): return result.astype(F32)  1.5 us

profile of v2, /device:TPU:24, one launch (start us, length us, event | category | flops | bytes accessed | tf_op | source)
XLA Modules:
  0.0 35.8 jit_solution(15889956967016699026)
XLA Ops:
  0.7 33.7 %shard_map.100 = bf16[64,512]{1,0:T(8,128)(2,1)} custom-call(f32[8,384]{1,0:T(8,128)} %decay_hbm.1, f32[384,512]{1,0:T(8,128)} %x_hbm.1, f32[384,128]{1,0:T(8,128)} %b_hbm.1, s32[1,1]{1,0:T(1,128)} %bitcast.3.counts_hbm, s32[1,128]{1,0:T(1,128)} %bound_hbm.1, f32[384,128]{1,0:T(8,128)} %c_hbm.1, f32[1,8]{1,0:T(1,128)} %bitcast.5, ...), custom_call_target="tpu_custom_call" | custom-call | tf_op jit(solution)/shard_map/pallas_call | solution.py:677
  34.3 1.5 %convert_element_type.3 = f32[64,512]{1,0:T(8,128)} convert(bf16[64,512]{1,0:T(8,128)(2,1)} %shard_map.100) | non-fusion elementwise | flops 32768 | bytes 196608 | tf_op jit(solution)/shard_map/convert_element_type | solution.py:715

commit v3 on v2

--- a/solution.py
+++ b/solution.py
@@ -209,6 +209,10 @@
     recv_a,
     send_b,
     recv_b,
+    send_w,
+    recv_w,
+    send_x,
+    recv_x,
     send_p,
     recv_p,
     recv_n,
@@ -222,6 +226,9 @@
     a_recv,
     b_send,
     b_recv,
+    w_sem,
+    x_send,
+    x_recv,
     p_send,
     p_recv,
     n_sem,
@@ -241,10 +248,10 @@
     state = b_ref.shape[1]
     slots = bound_ref.shape[1]
     rows = out_ref.shape[0]
-    piece = rows // groups
     half = rows // 2
     lo = (seqs - pairs) // 2
     is_owner = (me >= lo) & (me < lo + pairs)
+    has_below, has_above = me > 0, me < seqs - 1
 
     def shard_at(d):
         return lax.rem(me + d + seqs, seqs)
@@ -268,13 +275,13 @@
         return lax.rem(col + d, groups)
 
     chip = col // 2
-    partner = 2 * chip + 1 - lax.rem(col, 2)
+    core = lax.rem(col, 2)
+    partner = 2 * chip + 1 - core
     other = 2 * (1 - chip)
 
     barrier = pltpu.get_barrier_semaphore()
     peers = [(shard_at(d), col) for d in range(1, seqs)]
     peers += [(me, head_at(d)) for d in range(1, groups)]
-    peers += [(shard_at(e), head_at(d)) for e in (-1, 1) for d in range(1, groups)]
     for peer in peers:
         pl.semaphore_signal(
             barrier, inc=1, device_id=peer, device_id_type=pl.DeviceIdType.MESH
@@ -349,7 +356,7 @@
     for k in range(pairs):
         j = jnp.where(near_end, pairs - 1 - k, k)
 
-        @pl.when(me != lo + j)
+        @pl.when((me != lo + j) & (me < seqs - 1))
         def _():
             a_copy(j, me).start()
 
@@ -359,11 +366,19 @@
     def _():
         recv_a[me] = send_a[me - lo]
 
+    @pl.when(me == 0)
+    def _():
+        recv_b[...] = jnp.zeros(recv_b.shape, recv_b.dtype)
+
     lower = (iota((length, length), 0) >= iota((length, length), 1)).astype(F32)
-    logs_t = -exact_dot(lower, decay, ((1,), (1,)))
-    first = iota((heads, width), 0) * lanes
-    channel = iota((heads, width), 1)
-    spread = ((channel >= first) & (channel < first + lanes)).astype(F32)
+    twice = [decay, decay, jnp.zeros((state - 2 * heads, length), F32)]
+    logs_t = -exact_dot(lower, jnp.concatenate(twice, axis=0), ((1,), (1,)))
+    lane = iota((state, width), 0)
+    first = lax.rem(lane, heads) * lanes
+    channel = iota((state, width), 1)
+    spread = (channel >= first) & (channel < first + lanes)
+    spread_one = (spread & (lane < heads)).astype(F32)
+    spread_two = (spread & (lane < 2 * heads)).astype(BF16)
     for load in loads[4:7]:
         load.wait()
     marks = jnp.broadcast_to(bound_ref[...].astype(F32), (slots, slots)).T
@@ -391,142 +406,56 @@
             )
         inside.append(jnp.where(first_lane, parts[0], parts[1]))
     inside = jnp.concatenate(inside, axis=1)
-    enter_scale = exact_dot(jnp.exp(logs_sel), spread)
-    c_high, c_low = halves(c_rows)
+    enter = jnp.exp(logs_sel)
+    e_high = enter.astype(BF16).astype(F32)
+    enter_lane = iota((slots, state), 1)
+    e_pack = jnp.where(enter_lane < heads, e_high, enter - e_high)
+    e_pack = jnp.where(enter_lane < 2 * heads, e_pack, 0.0).astype(BF16)
+    sel = jnp.concatenate([*halves(inside), *halves(c_rows), e_pack], axis=1)
 
     for d in range(1, seqs):
         source = shard_at(-d)
         tag_copy(shard_at(d), source, source).wait_recv()
     all_tags = tag_recv[...].reshape(seqs, state)
     tag_lane = iota((seqs, state), 1)
-
-    def b_copy(s, j):
-        return remote(send_b.at[s], recv_b.at[j], b_send.at[s], b_recv.at[j], (s, col))
-
-    @pl.when(is_owner)
-    def _():
-        mine = me - lo
-        even = jnp.sum(jnp.where(tag_lane == 2 * mine, all_tags, 0.0), axis=1, keepdims=True)
-        odd = jnp.sum(jnp.where(tag_lane == 2 * mine + 1, all_tags, 0.0), axis=1, keepdims=True)
-        kept = jnp.exp(jnp.where(iota((seqs, pair_width), 1) < lanes, even, odd))
-        running = jnp.zeros((state, pair_width), F32)
-        for s in range(seqs):
-            send_b[s] = running.astype(BF16)
-
-            @pl.when(me != s)
-            def _():
-                b_copy(s, mine).start()
-
-            if s < seqs - 1:
-
-                @pl.when(me != s)
-                def _():
-                    a_copy(mine, s).wait_recv()
-
-                running = kept[s : s + 1] * running + recv_a[s].astype(F32)
-
-        @pl.when(me != seqs - 1)
-        def _():
-            a_copy(mine, seqs - 1).wait_recv()
-
-        recv_b[mine] = send_b[me]
-
-    earlier = (iota((seqs, state), 0) < me) & (tag_lane == heads)
+    tag_shard = iota((seqs, state), 0)
+    earlier = (tag_shard < me) & (tag_lane == heads)
     start = jnp.sum(jnp.where(earlier, all_tags, 0.0), axis=(0, 1), keepdims=True)
     offset = start - (me * rows - half).astype(F32)
     slot = iota((slots, slots), 1).astype(F32)
     count = jnp.broadcast_to(counts_ref[...].astype(F32), (slots, slots))
     shift = (slot == iota((slots, slots), 0).astype(F32) - offset) & (slot < count)
-    shift = shift.astype(BF16)
-
-    for j in range(pairs):
-
-        @pl.when(me != lo + j)
-        def _():
-            b_copy(me, j).wait_recv()
-
-    entering = jnp.concatenate([recv_b[j] for j in range(pairs)], axis=1)
-    carried = fast_dot(c_high, entering) + fast_dot(c_low, entering)
-    y = (inside + enter_scale * carried).astype(BF16)
-    window = fast_dot(shift, y).astype(BF16)
-    loads[7].wait()
-    partial = fast_dot(window, outw[...])
-    pieces = slots // piece
-    for i in range(pieces):
-        send_p[i] = partial[i * piece : (i + 1) * piece, :].astype(BF16)
-    outer = (pieces - groups) // 2
-
-    def project(src, slot, k, peer):
-        return remote(send_p.at[src], recv_p.at[slot], p_send.at[k], p_recv.at[slot], peer)
-
-    below_sent = [project(i, groups + col, i, (shard_at(-1), groups - outer + i)) for i in range(outer)]
-    above_sent = [
-        project(outer + groups + i, groups + col, outer + i, (shard_at(1), i))
-        for i in range(outer)
-    ]
-    sent = []
-    for d in range(1, groups):
-        to = head_at(d)
-        sent.append(project(outer + to, col, 2 * outer + d - 1, (me, to)))
-    has_below, has_above = me > 0, me < seqs - 1
+    window = fast_dot(shift.astype(BF16), sel)
+    send_w[...] = jnp.concatenate(
+        [window[:rows, :width], window[:rows, 2 * width :]], axis=1
+    ).astype(BF16)
+
+    w_copy = remote(send_w, recv_w, w_sem.at[0], w_sem.at[1], (shard_at(-1), col))
 
     @pl.when(has_below)
     def _():
-        for copy in below_sent:
-            copy.start()
-
-    @pl.when(has_above)
-    def _():
-        for copy in above_sent:
-            copy.start()
-
-    for copy in sent:
-        copy.start()
-    recv_p[col] = send_p[outer + col]
-    expects = (has_below & (col < outer)) | (has_above & (col >= outer))
-
-    @pl.when(expects)
-    def _():
-        for k in range(groups):
-            project(0, groups + k, 0, (shard_at(1), k)).wait_recv()
-
-    @pl.when(jnp.logical_not(expects))
-    def _():
-        recv_p[groups:] = jnp.zeros((groups, piece, recv_p.shape[2]), recv_p.dtype)
-
-    for d in range(1, groups):
-        source = head_at(groups - d)
-        project(0, source, 0, (me, source)).wait_recv()
-    loads[8].wait()
-    mixed = recv_p[0].astype(F32)
-    for k in range(1, 2 * groups):
-        mixed = mixed + recv_p[k].astype(F32)
-    square = jnp.mean(mixed * mixed, axis=-1, keepdims=True)
-    normed = (mixed * lax.rsqrt(square + 1e-05) * gain_ref[...]).astype(BF16)
-    recv_n[col] = normed
-
-    def n_copy(to, source):
-        return remote(recv_n.at[col], recv_n.at[source], n_sem.at[0, to], n_sem.at[1, source], (me, to))
-
-    sent_n = [n_copy(to, col) for to in (other, other + 1, partner)]
-    for copy in sent_n:
-        copy.start()
-    loads[9].wait()
-    near = rows // CHUNKS
-
-    def q_copy(j, slot, part):
+        w_copy.start()
+
+    @pl.when(jnp.logical_not(has_above))
+    def _():
+        recv_w[...] = jnp.zeros(recv_w.shape, recv_w.dtype)
+
+    for load in loads[7:]:
+        load.wait()
+
+    def norm(parts):
+        mixed = parts[0].astype(F32)
+        for k in range(1, groups):
+            mixed = mixed + parts[k].astype(F32)
+        square = jnp.mean(mixed * mixed, axis=-1, keepdims=True)
+        return (mixed * lax.rsqrt(square + 1e-05) * gain_ref[...]).astype(BF16)
+
+    def q_copy(j, block, part):
         return remote(
-            send_q.at[j, part],
-            recv_q.at[slot, part],
-            q_send.at[part, j],
-            q_recv.at[part, slot],
-            (lo + j, col),
+            send_q.at[j, part], recv_q.at[block], q_send.at[part, j], q_recv.at[block], (lo + j, col)
         )
 
-    for sources, part in (((partner,), chip), ((other, other + 1), 1 - chip)):
-        for source in sources:
-            n_copy(source, source).wait_recv()
-        block = recv_n[pl.ds(2 * part, 2)].reshape(near, -1)
+    def spread_out(block, to, part):
         for i in range(3):
             product = fast_dot(block, qkvw[i]).astype(BF16)
             for pair in range(pairs):
@@ -534,29 +463,139 @@
         for k in range(pairs):
             j = jnp.where(near_end, pairs - 1 - k, k)
 
-            @pl.when(me != lo + j)
+            @pl.when((me != lo + j) & (to < 2 * seqs))
             def _():
-                q_copy(j, me, part).start()
-
-    def attend(queries, keys, values, first_row):
+                q_copy(j, to, part).start()
+
+    def x_copy(k, slot, to):
+        return remote(send_x, recv_x.at[slot], x_send.at[k], x_recv.at[slot], (me, to))
+
+    @pl.when(me == 0)
+    def _():
+        early = window[half:rows, :width] + window[half:rows, width : 2 * width]
+        send_x[...] = fast_dot(early.astype(BF16), outw[...]).astype(BF16)
+        for k, to in enumerate((other, other + 1, partner)):
+            x_copy(k, col, to).start()
+        recv_x[col] = send_x[...]
+        for k, source in enumerate((partner, other, other + 1)):
+            x_copy(0, source, source).wait_recv()
+        spread_out(norm(recv_x), 0, 2)
+
+    def b_copy(s, j):
+        return remote(send_b.at[s], recv_b.at[j], b_send.at[s], b_recv.at[j], (s, col))
+
+    @pl.when(is_owner)
+    def _():
+        mine = me - lo
+        even = jnp.sum(jnp.where(tag_lane == 2 * mine, all_tags, 0.0), axis=1, keepdims=True)
+        odd = jnp.sum(jnp.where(tag_lane == 2 * mine + 1, all_tags, 0.0), axis=1, keepdims=True)
+        kept = jnp.exp(jnp.where(iota((seqs, pair_width), 1) < lanes, even, odd))
+        running = jnp.zeros((state, pair_width), F32)
+        for s in range(1, seqs):
+
+            @pl.when(me != s - 1)
+            def _():
+                a_copy(mine, s - 1).wait_recv()
+
+            running = kept[s - 1 : s] * running + recv_a[s - 1].astype(F32)
+            send_b[s] = running.astype(BF16)
+
+            @pl.when(me != s)
+            def _():
+                b_copy(s, mine).start()
+
+        recv_b[mine] = send_b[me]
+
+    spans = jnp.exp(jnp.where(tag_lane < heads, all_tags, 0.0))
+    here = jnp.sum(jnp.where(tag_shard == me, spans, 0.0), axis=0, keepdims=True)
+    span_here = exact_dot(jnp.broadcast_to(here, (heads, state)), spread_one)[0:1]
+    owned = window[rows:]
+    mine_scale = fast_dot(owned[:, 2 * width + 2 * state :].astype(BF16), spread_two)
+
+    @pl.when(has_above)
+    def _():
+        w_copy.wait_recv()
+
+    near_rows = recv_w[...].astype(F32)
+    near_scale = fast_dot(recv_w[:, width + 2 * state :], spread_two)
+    c_both = owned[:, 2 * width : 2 * width + 2 * state] + near_rows[:, width : width + 2 * state]
+    c_stack = jnp.concatenate([c_both[:, :state], c_both[:, state:]], axis=0).astype(BF16)
+
+    def through(ref):
+        wide = fast_dot(c_stack, jnp.concatenate([ref[j] for j in range(pairs)], axis=1))
+        return wide[:rows] + wide[rows:]
+
+    reach = owned[:, :width] + owned[:, width : 2 * width] + near_rows[:, :width]
+    reach = reach + near_scale * through(send_a)
+    far_scale = mine_scale + span_here * near_scale
+
+    for j in range(pairs):
+
+        @pl.when(has_below & (me != lo + j))
+        def _():
+            b_copy(me, j).wait_recv()
+
+    y = (reach + far_scale * through(recv_b)).astype(BF16)
+    partial = fast_dot(y, outw[...]).astype(BF16)
+    for part in range(CHUNKS):
+        send_p[part] = partial[part * half : (part + 1) * half]
+
+    def p_copy(src, slot, k, to):
+        return remote(send_p.at[src], recv_p.at[slot], p_send.at[k], p_recv.at[slot], (me, to))
+
+    sent = [
+        p_copy(0, col, 0, other),
+        p_copy(1, col, 1, other + 1),
+        p_copy(1 - core, col, 2, partner),
+    ]
+    for copy in sent:
+        copy.start()
+    recv_p[col] = send_p[core]
+    for source in (partner, other, other + 1):
+        p_copy(0, source, 0, source).wait_recv()
+    normed = norm(recv_p)
+    recv_n[core] = normed
+
+    def n_copy(slot):
+        return remote(recv_n.at[core], recv_n.at[slot], n_sem.at[0], n_sem.at[1], (me, partner))
+
+    n_copy(core).start()
+    spread_out(normed, 2 * me + 1 + core, core)
+    n_copy(1 - core).wait_recv()
+    spread_out(recv_n[1 - core], 2 * me + 2 - core, 1 - core)
+
+    def attend(queries, keys, values):
+        count, seen_before = queries.shape[0], keys.shape[0] - queries.shape[0]
         left = iota(queries.shape, 1) < lanes
-        results = []
-        for keep in (left, jnp.logical_not(left)):
-            masked = jnp.where(keep, queries.astype(F32), 0.0).astype(BF16)
-            scores = fast_dot(masked, keys, ((1,), (1,))) * (lanes ** (-0.5))
-            allowed = first_row + iota(scores.shape, 0) >= iota(scores.shape, 1)
-            scores = jnp.where(allowed, scores, -1e30)
-            highest = jnp.max(scores, axis=-1, keepdims=True)
-            exps = jnp.where(allowed, jnp.exp(scores - highest), 0.0)
-            total = jnp.sum(exps, axis=-1, keepdims=True)
-            results.append(fast_dot(exps.astype(BF16), values) / total)
-        return jnp.where(left, results[0], results[1]).astype(BF16)
+        scaled = queries.astype(F32) * (lanes ** (-0.5))
+        heads_apart = [jnp.where(left, scaled, 0.0), jnp.where(left, 0.0, scaled)]
+        stacked = jnp.concatenate(heads_apart, axis=0).astype(BF16)
+        scores = fast_dot(stacked, keys, ((1,), (1,)))
+        corner = (2 * count, count)
+        row = iota(corner, 0)
+        row = jnp.where(row < count, row, row - count)
+        last = jnp.where(row >= iota(corner, 1), scores[:, seen_before:], -1e30)
+        highest = jnp.max(last, axis=-1, keepdims=True)
+        if seen_before:
+            first = scores[:, :seen_before]
+            highest = jnp.maximum(highest, jnp.max(first, axis=-1, keepdims=True))
+        exps = jnp.exp(last - highest)
+        total = jnp.sum(exps, axis=-1, keepdims=True)
+        result = fast_dot(exps.astype(BF16), values[seen_before:])
+        if seen_before:
+            exps = jnp.exp(first - highest)
+            total = total + jnp.sum(exps, axis=-1, keepdims=True)
+            result = result + fast_dot(exps.astype(BF16), values[:seen_before])
+        result = result / total
+        return jnp.where(left, result[:count], result[count:]).astype(BF16)
 
     @pl.when(me == 0)
     def _():
         for pair in range(pairs):
-            q, k, v = [send_q[pair, :, i].reshape(rows, pair_width) for i in range(3)]
-            first_out[:, pair * pair_width : (pair + 1) * pair_width] = attend(q, k, v, 0)
+            q, k, v = [
+                jnp.concatenate([send_q[pair, 2, i], send_q[pair, 0, i]], axis=0) for i in range(3)
+            ]
+            first_out[:, pair * pair_width : (pair + 1) * pair_width] = attend(q, k, v)
         pltpu.make_async_copy(first_out, out_ref, out_sem).start()
 
     def o_copy(s, j):
@@ -570,15 +609,19 @@
     @pl.when(is_owner)
     def _():
         mine = me - lo
-        recv_q[me] = send_q[mine]
-        for part in (chip, 1 - chip):
-            for d in range(1, seqs):
-                q_copy(mine, shard_at(-d), part).wait_recv()
-        q, k, v = [recv_q[:, :, i].reshape(seqs * rows, pair_width) for i in range(3)]
+        for part in range(CHUNKS):
+            recv_q[2 * me + 1 + part] = send_q[mine, part]
+        for block in range(2 * seqs):
+
+            @pl.when(me != max(block - 1, 0) // 2)
+            def _():
+                q_copy(mine, block, 0).wait_recv()
+
+        q, k, v = [recv_q[:, i].reshape(seqs * rows, pair_width) for i in range(3)]
         span = 2 * rows
-        for n in range(seqs // 2):
+        for n in [0, seqs // 2 - 1, *range(1, seqs // 2 - 1)]:
             end = (n + 1) * span
-            result = attend(q[n * span : end], k[:end], v[:end], n * span)
+            result = attend(q[n * span : end], k[:end], v[:end])
             for s in (2 * n, 2 * n + 1):
                 if s == 0:
                     continue
@@ -601,41 +644,44 @@
         def _():
             o_copy(me, j).wait_recv()
 
-    for copy in sent + sent_n:
+    for copy in sent:
         copy.wait_send()
+    n_copy(core).wait_send()
 
     @pl.when(has_below)
     def _():
-        for copy in below_sent:
-            copy.wait_send()
-
-    @pl.when(has_above)
-    def _():
-        for copy in above_sent:
-            copy.wait_send()
+        w_copy.wait_send()
+
+    @pl.when(me == 0)
+    def _():
+        for k in range(3):
+            x_copy(k, col, partner).wait_send()
+        for j in range(pairs):
+            q_copy(j, 0, 2).wait_send()
 
     for j in range(pairs):
+
+        @pl.when((me != lo + j) & (me < seqs - 1))
+        def _():
+            a_copy(j, me).wait_send()
 
         @pl.when(me != lo + j)
         def _():
-            a_copy(j, me).wait_send()
-            for part in range(CHUNKS):
-                q_copy(j, me, part).wait_send()
+            q_copy(j, 0, 0).wait_send()
+
+        @pl.when((me != lo + j) & has_above)
+        def _():
+            q_copy(j, 0, 1).wait_send()
 
     for to in targets:
         tag_copy(to, me, me).wait_send()
 
-    for s in range(seqs):
+    for s in range(1, seqs):
 
         @pl.when(is_owner & (me != s))
         def _():
             b_copy(s, me - lo).wait_send()
-
-        if s > 0:
-
-            @pl.when(is_owner & (me != s))
-            def _():
-                o_copy(s, me - lo).wait_send()
+            o_copy(s, me - lo).wait_send()
 
 
 def fused_body(
@@ -657,9 +703,8 @@
     pairs = heads // 2
     state = b_proj.shape[1]
     rows = ROWS_DEV
-    piece = rows // groups
+    half = rows // 2
     enc = out_weight.shape[1]
-    pieces = boundaries.shape[1] // piece
     hbm = pl.BlockSpec(memory_space=pl.ANY)
     dma = pltpu.SemaphoreType.DMA
     operands = (
@@ -688,11 +733,15 @@
             pltpu.VMEM((seqs, state, 2 * lanes), BF16),
             pltpu.VMEM((seqs, state, 2 * lanes), BF16),
             pltpu.VMEM((pairs, state, 2 * lanes), BF16),
-            pltpu.VMEM((pieces, piece, enc), BF16),
-            pltpu.VMEM((2 * groups, piece, enc), BF16),
-            pltpu.VMEM((groups, piece, enc), BF16),
-            pltpu.VMEM((pairs, CHUNKS, 3, rows // CHUNKS, 2 * lanes), BF16),
-            pltpu.VMEM((seqs, CHUNKS, 3, rows // CHUNKS, 2 * lanes), BF16),
+            pltpu.VMEM((rows, width + 3 * state), BF16),
+            pltpu.VMEM((rows, width + 3 * state), BF16),
+            pltpu.VMEM((half, enc), BF16),
+            pltpu.VMEM((groups, half, enc), BF16),
+            pltpu.VMEM((CHUNKS, half, enc), BF16),
+            pltpu.VMEM((groups, half, enc), BF16),
+            pltpu.VMEM((CHUNKS, half, enc), BF16),
+            pltpu.VMEM((pairs, CHUNKS + 1, 3, half, 2 * lanes), BF16),
+            pltpu.VMEM((seqs * CHUNKS, 3, half, 2 * lanes), BF16),
             pltpu.VMEM((seqs, rows, 2 * lanes), BF16),
             pltpu.VMEM((rows, width), BF16),
             dma((len(operands),)),
@@ -701,11 +750,14 @@
             dma((seqs,)),
             dma((seqs,)),
             dma((pairs,)),
-            dma((2 * groups,)),
-            dma((2 * groups,)),
-            dma((2, groups)),
-            dma((CHUNKS, pairs)),
-            dma((CHUNKS, seqs)),
+            dma((2,)),
+            dma((groups,)),
+            dma((groups,)),
+            dma((groups,)),
+            dma((groups,)),
+            dma((2,)),
+            dma((CHUNKS + 1, pairs)),
+            dma((CHUNKS * seqs,)),
             dma((seqs,)),
             dma((pairs,)),
             dma,

time: 36 us -> 33.1 us (0.919)
  the two profiles are of different devices: /device:TPU:24 before, /device:TPU:8 now
where the time goes in v3:
time: 33.1 us; the launch traced here: 32.8 us
  Pallas kernels  30.7 us (93%)
  other arithmetic  1.5 us (5%)
  between operations  0.66 us (2%)
    pallas_call x1, Pallas kernels, fused_body(): pl.pallas_call(functools.partial(fused, seqs, groups), out_shape=jax.Shap...  30.7 us
    convert_element_type x1, other arithmetic, fused_body(): return result.astype(F32)  1.5 us

profile of v3, /device:TPU:8, one launch (start us, length us, event | category | flops | bytes accessed | tf_op | source)
XLA Modules:
  0.0 32.8 jit_solution(12222847016678319524)
XLA Ops:
  0.7 30.7 %shard_map.100 = bf16[64,512]{1,0:T(8,128)(2,1)} custom-call(f32[8,384]{1,0:T(8,128)} %decay_hbm.1, f32[384,512]{1,0:T(8,128)} %x_hbm.1, f32[384,128]{1,0:T(8,128)} %b_hbm.1, s32[1,1]{1,0:T(1,128)} %bitcast.3.counts_hbm, s32[1,128]{1,0:T(1,128)} %bound_hbm.1, f32[384,128]{1,0:T(8,128)} %c_hbm.1, f32[1,8]{1,0:T(1,128)} %bitcast.5, ...), custom_call_target="tpu_custom_call" | custom-call | tf_op jit(solution)/shard_map/pallas_call | solution.py:722
  31.3 1.5 %convert_element_type.3 = f32[64,512]{1,0:T(8,128)} convert(bf16[64,512]{1,0:T(8,128)(2,1)} %shard_map.100) | non-fusion elementwise | flops 32768 | bytes 196608 | tf_op jit(solution)/shard_map/convert_element_type | solution.py:767

commit v4 on v3

--- a/solution.py
+++ b/solution.py
@@ -477,9 +477,6 @@
         for k, to in enumerate((other, other + 1, partner)):
             x_copy(k, col, to).start()
         recv_x[col] = send_x[...]
-        for k, source in enumerate((partner, other, other + 1)):
-            x_copy(0, source, source).wait_recv()
-        spread_out(norm(recv_x), 0, 2)
 
     def b_copy(s, j):
         return remote(send_b.at[s], recv_b.at[j], b_send.at[s], b_recv.at[j], (s, col))
@@ -540,29 +537,50 @@
     for part in range(CHUNKS):
         send_p[part] = partial[part * half : (part + 1) * half]
 
-    def p_copy(src, slot, k, to):
-        return remote(send_p.at[src], recv_p.at[slot], p_send.at[k], p_recv.at[slot], (me, to))
-
-    sent = [
-        p_copy(0, col, 0, other),
-        p_copy(1, col, 1, other + 1),
-        p_copy(1 - core, col, 2, partner),
-    ]
-    for copy in sent:
-        copy.start()
-    recv_p[col] = send_p[core]
-    for source in (partner, other, other + 1):
-        p_copy(0, source, 0, source).wait_recv()
-    normed = norm(recv_p)
-    recv_n[core] = normed
-
-    def n_copy(slot):
-        return remote(recv_n.at[core], recv_n.at[slot], n_sem.at[0], n_sem.at[1], (me, partner))
-
-    n_copy(core).start()
-    spread_out(normed, 2 * me + 1 + core, core)
-    n_copy(1 - core).wait_recv()
-    spread_out(recv_n[1 - core], 2 * me + 2 - core, 1 - core)
+    def p_copy(part, slot, k, to):
+        return remote(
+            send_p.at[part], recv_p.at[part, slot], p_send.at[part, k], p_recv.at[part, slot], (me, to)
+        )
+
+    for part in range(CHUNKS):
+        p_copy(part, col, 0, other).start()
+
+    @pl.when(core == 1)
+    def _():
+        for part in range(CHUNKS):
+            p_copy(part, col, 1, partner).start()
+
+    @pl.when(core == 0)
+    def _():
+        for part in range(CHUNKS):
+            recv_p[part, col] = send_p[part]
+
+    @pl.when(me == 0)
+    def _():
+        for source in (partner, other, other + 1):
+            x_copy(0, source, source).wait_recv()
+        spread_out(norm(recv_x), 0, 2)
+
+    def n_copy(part):
+        return remote(
+            recv_n.at[part], recv_n.at[part], n_sem.at[0, part], n_sem.at[1, part], (me, partner)
+        )
+
+    @pl.when(core == 0)
+    def _():
+        for part in range(CHUNKS):
+            for source in (partner, other, other + 1):
+                p_copy(part, source, 0, source).wait_recv()
+            normed = norm(recv_p[part])
+            recv_n[part] = normed
+            n_copy(part).start()
+            spread_out(normed, 2 * me + 1 + part, part)
+
+    @pl.when(core == 1)
+    def _():
+        for part in range(CHUNKS):
+            n_copy(part).wait_recv()
+            spread_out(recv_n[part], 2 * me + 1 + part, part)
 
     def attend(queries, keys, values):
         count, seen_before = queries.shape[0], keys.shape[0] - queries.shape[0]
@@ -611,17 +629,20 @@
         mine = me - lo
         for part in range(CHUNKS):
             recv_q[2 * me + 1 + part] = send_q[mine, part]
-        for block in range(2 * seqs):
-
-            @pl.when(me != max(block - 1, 0) // 2)
-            def _():
-                q_copy(mine, block, 0).wait_recv()
-
-        q, k, v = [recv_q[:, i].reshape(seqs * rows, pair_width) for i in range(3)]
         span = 2 * rows
-        for n in [0, seqs // 2 - 1, *range(1, seqs // 2 - 1)]:
-            end = (n + 1) * span
-            result = attend(q[n * span : end], k[:end], v[:end])
+        step = span // half
+        arrived = 0
+        for n in range(seqs // 2):
+            for block in range(arrived, step * (n + 1)):
+
+                @pl.when(me != max(block - 1, 0) // 2)
+                def _():
+                    q_copy(mine, block, 0).wait_recv()
+
+            arrived = max(arrived, step * (n + 1))
+            q = recv_q[step * n : step * (n + 1), 0].reshape(span, pair_width)
+            k, v = [recv_q[: step * (n + 1), i].reshape((n + 1) * span, pair_width) for i in (1, 2)]
+            result = attend(q, k, v)
             for s in (2 * n, 2 * n + 1):
                 if s == 0:
                     continue
@@ -644,9 +665,16 @@
         def _():
             o_copy(me, j).wait_recv()
 
-    for copy in sent:
-        copy.wait_send()
-    n_copy(core).wait_send()
+    for part in range(CHUNKS):
+        p_copy(part, col, 0, other).wait_send()
+
+        @pl.when(core == 1)
+        def _():
+            p_copy(part, col, 1, partner).wait_send()
+
+        @pl.when(core == 0)
+        def _():
+            n_copy(part).wait_send()
 
     @pl.when(has_below)
     def _():
@@ -738,7 +766,7 @@
             pltpu.VMEM((half, enc), BF16),
             pltpu.VMEM((groups, half, enc), BF16),
             pltpu.VMEM((CHUNKS, half, enc), BF16),
-            pltpu.VMEM((groups, half, enc), BF16),
+            pltpu.VMEM((CHUNKS, groups, half, enc), BF16),
             pltpu.VMEM((CHUNKS, half, enc), BF16),
             pltpu.VMEM((pairs, CHUNKS + 1, 3, half, 2 * lanes), BF16),
             pltpu.VMEM((seqs * CHUNKS, 3, half, 2 * lanes), BF16),
@@ -753,9 +781,9 @@
             dma((2,)),
             dma((groups,)),
             dma((groups,)),
-            dma((groups,)),
-            dma((groups,)),
-            dma((2,)),
+            dma((CHUNKS, 2)),
+            dma((CHUNKS, groups)),
+            dma((2, CHUNKS)),
             dma((CHUNKS + 1, pairs)),
             dma((CHUNKS * seqs,)),
             dma((seqs,)),

time: 33.1 us -> 31.8 us (0.961)
  the two profiles are of different devices: /device:TPU:8 before, /device:TPU:24 now
where the time goes in v4:
time: 31.8 us; the launch traced here: 31.5 us
  Pallas kernels  29.3 us (92%)
  other arithmetic  1.5 us (5%)
  between operations  0.66 us (2%)
    pallas_call x1, Pallas kernels, fused_body(): pl.pallas_call(functools.partial(fused, seqs, groups), out_shape=jax.Shap...  29.3 us
    convert_element_type x1, other arithmetic, fused_body(): return result.astype(F32)  1.5 us

profile of v4, /device:TPU:24, one launch (start us, length us, event | category | flops | bytes accessed | tf_op | source)
XLA Modules:
  0.0 31.5 jit_solution(2533869265377615475)
XLA Ops:
  0.7 29.3 %shard_map.100 = bf16[64,512]{1,0:T(8,128)(2,1)} custom-call(f32[8,384]{1,0:T(8,128)} %decay_hbm.1, f32[384,512]{1,0:T(8,128)} %x_hbm.1, f32[384,128]{1,0:T(8,128)} %b_hbm.1, s32[1,1]{1,0:T(1,128)} %bitcast.3.counts_hbm, s32[1,128]{1,0:T(1,128)} %bound_hbm.1, f32[384,128]{1,0:T(8,128)} %c_hbm.1, f32[1,8]{1,0:T(1,128)} %bitcast.5, ...), custom_call_target="tpu_custom_call" | custom-call | tf_op jit(solution)/shard_map/pallas_call | solution.py:750
  29.9 1.5 %convert_element_type.3 = f32[64,512]{1,0:T(8,128)} convert(bf16[64,512]{1,0:T(8,128)(2,1)} %shard_map.100) | non-fusion elementwise | flops 32768 | bytes 196608 | tf_op jit(solution)/shard_map/convert_element_type | solution.py:795

commit v5 on v4

--- a/solution.py
+++ b/solution.py
@@ -425,10 +425,9 @@
     slot = iota((slots, slots), 1).astype(F32)
     count = jnp.broadcast_to(counts_ref[...].astype(F32), (slots, slots))
     shift = (slot == iota((slots, slots), 0).astype(F32) - offset) & (slot < count)
-    window = fast_dot(shift.astype(BF16), sel)
-    send_w[...] = jnp.concatenate(
-        [window[:rows, :width], window[:rows, 2 * width :]], axis=1
-    ).astype(BF16)
+    shift = shift.astype(BF16)
+    passed = jnp.concatenate([sel[:, :width], sel[:, 2 * width :]], axis=1)
+    send_w[...] = fast_dot(shift[:rows], passed).astype(BF16)
 
     w_copy = remote(send_w, recv_w, w_sem.at[0], w_sem.at[1], (shard_at(-1), col))
 
@@ -472,11 +471,14 @@
 
     @pl.when(me == 0)
     def _():
-        early = window[half:rows, :width] + window[half:rows, width : 2 * width]
+        early = fast_dot(shift[half:rows], sel[:, : 2 * width])
+        early = early[:, :width] + early[:, width:]
         send_x[...] = fast_dot(early.astype(BF16), outw[...]).astype(BF16)
         for k, to in enumerate((other, other + 1, partner)):
             x_copy(k, col, to).start()
         recv_x[col] = send_x[...]
+
+    owned = fast_dot(shift[rows:], sel)
 
     def b_copy(s, j):
         return remote(send_b.at[s], recv_b.at[j], b_send.at[s], b_recv.at[j], (s, col))
@@ -506,7 +508,6 @@
     spans = jnp.exp(jnp.where(tag_lane < heads, all_tags, 0.0))
     here = jnp.sum(jnp.where(tag_shard == me, spans, 0.0), axis=0, keepdims=True)
     span_here = exact_dot(jnp.broadcast_to(here, (heads, state)), spread_one)[0:1]
-    owned = window[rows:]
     mine_scale = fast_dot(owned[:, 2 * width + 2 * state :].astype(BF16), spread_two)
 
     @pl.when(has_above)

time: 31.8 us -> 31.8 us (level)
  no operation moved by 1% of the time
where the time goes in v5:
time: 31.8 us; the launch traced here: 31.4 us
  Pallas kernels  29.2 us (92%)
  other arithmetic  1.5 us (5%)
  between operations  0.66 us (2%)
    pallas_call x1, Pallas kernels, fused_body(): pl.pallas_call(functools.partial(fused, seqs, groups), out_shape=jax.Shap...  29.2 us
    convert_element_type x1, other arithmetic, fused_body(): return result.astype(F32)  1.5 us

profile of v5, /device:TPU:24, one launch (start us, length us, event | category | flops | bytes accessed | tf_op | source)
XLA Modules:
  0.0 31.4 jit_solution(17790113502487818392)
XLA Ops:
  0.7 29.2 %shard_map.100 = bf16[64,512]{1,0:T(8,128)(2,1)} custom-call(f32[8,384]{1,0:T(8,128)} %decay_hbm.1, f32[384,512]{1,0:T(8,128)} %x_hbm.1, f32[384,128]{1,0:T(8,128)} %b_hbm.1, s32[1,1]{1,0:T(1,128)} %bitcast.3.counts_hbm, s32[1,128]{1,0:T(1,128)} %bound_hbm.1, f32[384,128]{1,0:T(8,128)} %c_hbm.1, f32[1,8]{1,0:T(1,128)} %bitcast.5, ...), custom_call_target="tpu_custom_call" | custom-call | tf_op jit(solution)/shard_map/pallas_call | solution.py:751
  29.9 1.5 %convert_element_type.3 = f32[64,512]{1,0:T(8,128)} convert(bf16[64,512]{1,0:T(8,128)(2,1)} %shard_map.100) | non-fusion elementwise | flops 32768 | bytes 196608 | tf_op jit(solution)/shard_map/convert_element_type | solution.py:796
